TPU v7x, 128 devices: a whole 4x4x4 slice. The times are simulated.
128 devices in a mesh: lat: 4 (over y), lon: 4 (over z), mesh: 8 (over x, core).
Axes of the slice: x: 4, y: 4, z: 4, core: 2. Of those that a mesh axis runs over, the one named last changes fastest.
Arguments:
- grid_latent: bfloat16 [131072, 512], P(('lat', 'lon', 'mesh')), may hold values from -24 to 24
- target: bfloat16 [131072, 84], P(('lat', 'lon', 'mesh')), may hold values from -6 to 6
- area: float32 [131072], P(('lat', 'lon', 'mesh')), may hold values from 0.05 to 1
- mesh_latent: bfloat16 [40960, 512], P(('lat', 'lon', 'mesh')), may hold values from -6 to 6
- node_gain: float32 [512], replicated, may hold values from 0.1 to 1.9
- w_enc: bfloat16 [512, 512], replicated, may hold values from -0.25 to 0.25
- w_up: bfloat16 [512, 512], replicated, may hold values from -0.25 to 0.25
- w_down: bfloat16 [512, 512], replicated, may hold values from -0.25 to 0.25
- w_msg: bfloat16 [512, 512], replicated, may hold values from -0.25 to 0.25
- w_dec: bfloat16 [512, 512], replicated, may hold values from -0.25 to 0.25
- w_out: bfloat16 [512, 84], replicated, may hold values from -0.25 to 0.25
- enc_cell: int32 [128, 3, 3, 8, 21], P(('lat', 'lon', 'mesh')), may hold values from 0 to 1023
- enc_live: int32 [128, 3, 3, 8], P(('lat', 'lon', 'mesh')), may hold values from 1 to 21, as said below
- enc_weight: float32 [128, 3, 3, 8, 21], P(('lat', 'lon', 'mesh')), may hold values from 0.2 to 1
- enc_node: int32 [128, 3, 3, 8, 21], P(('lat', 'lon', 'mesh')), may hold values from 0 to 319
- dec_node: int32 [128, 3, 3, 8, 32], P(('lat', 'lon', 'mesh')), may hold values from 0 to 319
- dec_cell: int32 [128, 3, 3, 8, 32], P(('lat', 'lon', 'mesh')), may hold values from 0 to 1023
- dec_weight: float32 [128, 3, 3, 8, 32], P(('lat', 'lon', 'mesh')), may hold values from 0.2 to 1
Outputs:
- grid_grad: float32 [131072, 512], P(('lat', 'lon', 'mesh'))
- grad_enc: float32 [512, 512], P(('lat', 'lon', 'mesh'))
- grad_up: float32 [512, 512], P(('lat', 'lon', 'mesh'))
- grad_down: float32 [512, 512], P(('lat', 'lon', 'mesh'))
- grad_msg: float32 [512, 512], P(('lat', 'lon', 'mesh'))
- grad_dec: float32 [512, 512], P(('lat', 'lon', 'mesh'))
- grad_out: float32 [512, 84], P(('lat', 'lon', 'mesh'))
Inputs may be any that keep to these rules, and one draw needn't show every extreme that they name: Slots 0 to enc_live - 1 of a bucket are edges, the others padding; in every draw some mesh owner receives 21 live slots in every bucket addressed to it. `enc_cell`: local cell indices. `enc_node`: local node indices. `dec_node`: local node indices. `dec_cell`: local cell indices.
All inputs are finite; a program needn't handle non-finite values.
Results may differ from a plain program's by a relative error of at most 0.0085.
Values may be sent and summed in bfloat16 or wider, within the bound.
A program may use at most 128 MiB of HBM per device.

v0:
```python
import jax
import jax.numpy as jnp
from jax import lax
from jax.sharding import Mesh
from jax.sharding import PartitionSpec as P

MESH = ("mesh_0", "mesh_1")
LAT_LON_MESH = ("lat", "lon", "mesh_0", "mesh_1")


def extended_2(cells, sides, width):
    for axis, dim in sides:
        count = lax.axis_size(axis)
        head = lax.slice_in_dim(cells, 0, width, axis=dim)
        tail = lax.slice_in_dim(cells, cells.shape[dim] - width, cells.shape[dim], axis=dim)
        cells = jnp.concatenate(
            [
                lax.ppermute(tail, axis, [(i, (i + 1) % count) for i in range(count)]),
                cells,
                lax.ppermute(head, axis, [((i + 1) % count, i) for i in range(count)]),
            ],
            axis=dim,
        )
    return cells


def cut_along(array, dim, size):
    lengths = array.shape
    tiles = array.reshape(*lengths[:dim], size, lengths[dim] // size, *lengths[dim + 1 :])
    return jnp.moveaxis(tiles, dim, 0)


def summed_on_arrival(array, axis, dim):
    size = lax.axis_size(axis)
    tiles = lax.all_to_all(cut_along(array, dim, size), axis, 0, 0, tiled=True)
    return jnp.sum(tiles.astype(jnp.float32), axis=0)


def sum_in_two_steps(array, axes, dim):
    far, near = axes
    tiles = cut_along(array, dim, lax.axis_size(far))
    nearer = summed_on_arrival(tiles, near, dim + 1)
    arrived = lax.all_to_all(
        nearer.astype(jnp.bfloat16), far, split_axis=0, concat_axis=0, tiled=True
    )
    return arrived.astype(jnp.float32).sum(axis=0)


def side_by_side(arrays, axis, dim, along):
    widths = [a.shape[along] for a in arrays]
    both = jnp.concatenate(arrays, axis=along)
    out = sum_in_two_steps(both, axis, dim)
    return tuple(jnp.split(out, [sum(widths[:k]) for k in range(1, len(widths))], axis=along))


def matmul(left, right):
    return jnp.dot(left, right, preferred_element_type=jnp.float32)


def contract(left, right):
    return lax.dot_general(
        left, right, (((0,), (0,)), ((), ())), preferred_element_type=jnp.float32
    )


def silu_slope(argument):
    sigmoid_value = jax.nn.sigmoid(argument)
    return sigmoid_value * (1.0 + argument * (1.0 - sigmoid_value))


def node_forward(node_state, node_gain, w_up, w_down):
    inv_rms = lax.rsqrt(jnp.mean(node_state * node_state, axis=-1, keepdims=True) + 1e-05)
    normed = (node_state * inv_rms * node_gain).astype(jnp.bfloat16)
    activation = matmul(normed, w_up)
    hidden = jax.nn.silu(activation).astype(jnp.bfloat16)
    updated = node_state + matmul(hidden, w_down)
    return (updated, inv_rms, normed, activation, hidden)


def node_backward(
    back_node, node_state, node_gain, w_up, w_down, inv_rms, normed, activation, hidden
):
    back_node_half = back_node.astype(jnp.bfloat16)
    grad_down = contract(hidden, back_node_half)
    back_hidden = matmul(back_node_half, w_down.T)
    back_act = (back_hidden * silu_slope(activation)).astype(jnp.bfloat16)
    grad_up = contract(normed, back_act)
    back_norm = matmul(back_act, w_up.T) * node_gain
    mean_term = jnp.mean(node_state * back_norm, axis=-1, keepdims=True)
    back_state = back_node + inv_rms * back_norm - node_state * inv_rms**3 * mean_term
    return (back_state, grad_up, grad_down)


def route_enc(bucket):
    crossed = lax.all_to_all(bucket, MESH, split_axis=2, concat_axis=2, tiled=True)
    extended = extended_2(crossed, (("lat", 0), ("lon", 1)), 1)
    result = extended[::-2, ::-2]
    return result


def route_dec(bucket):
    crossed = lax.all_to_all(bucket, MESH, split_axis=2, concat_axis=2, tiled=True)
    extended = extended_2(crossed, (("lat", 0), ("lon", 1)), 1)
    result = extended[::-2, ::-2]
    return result


def on_device(
    grid_latent,
    target,
    area,
    mesh_latent,
    node_gain,
    w_enc,
    w_up,
    w_down,
    w_msg,
    w_dec,
    w_out,
    enc_cell,
    enc_live,
    enc_weight,
    enc_node,
    dec_node,
    dec_cell,
    dec_weight,
):
    cell_rows = grid_latent.shape[0]
    node_rows = mesh_latent.shape[0]
    features = grid_latent.shape[1]
    send_cells = enc_cell[0]
    offsets = jnp.arange(3, dtype=jnp.int32) - 1
    lat_here = lax.axis_index("lat")
    lat_count = lax.axis_size("lat")
    reach_up = lat_here + offsets
    send_ok = (reach_up >= 0) & (reach_up < lat_count)
    reach_down = lat_here - offsets
    recv_ok = (reach_down >= 0) & (reach_down < lat_count)
    slot_index = jnp.arange(send_cells.shape[-1], dtype=jnp.int32)
    edge_scale = jnp.where(
        (slot_index < enc_live[0][..., None]) & send_ok[:, None, None, None],
        enc_weight[0],
        jnp.float32(0.0),
    )
    dec_scale = jnp.where(recv_ok[:, None, None, None], dec_weight[0], jnp.float32(0.0))
    projected = matmul(grid_latent, w_enc).astype(jnp.bfloat16)
    outgoing = (edge_scale[..., None] * projected[send_cells].astype(jnp.float32)).astype(
        jnp.bfloat16
    )
    landed = route_enc(outgoing)
    aggregate = jax.ops.segment_sum(
        landed.reshape(-1, features).astype(jnp.float32),
        enc_node[0].reshape(-1),
        num_segments=node_rows,
    )
    node_state = mesh_latent.astype(jnp.float32) + aggregate
    updated, inv_rms, normed, activation, hidden = node_forward(node_state, node_gain, w_up, w_down)
    node_half = updated.astype(jnp.bfloat16)
    leaving = node_half[dec_node[0]]
    pulled = route_dec(leaving)
    row_block = pulled.reshape(-1, features)
    preact = matmul(row_block, w_msg)
    edge_weight = dec_scale.reshape(-1)[:, None]
    cell_ids = dec_cell[0].reshape(-1)
    weighted = edge_weight * jax.nn.silu(preact)
    gathered = jax.ops.segment_sum(weighted, cell_ids, num_segments=cell_rows).astype(jnp.bfloat16)
    blended = grid_latent.astype(jnp.float32) + matmul(gathered, w_dec)
    blended_half = blended.astype(jnp.bfloat16)
    output = matmul(blended_half, w_out)
    residual = (area[:, None] * (output - target.astype(jnp.float32))).astype(jnp.bfloat16)
    grad_out = contract(blended_half, residual) / cell_rows
    back_blend = matmul(residual, w_out.T)
    back_half = back_blend.astype(jnp.bfloat16)
    grad_dec = contract(gathered, back_half) / cell_rows
    back_gather = matmul(back_half, w_dec.T).astype(jnp.bfloat16)
    back_message = edge_weight * back_gather[cell_ids].astype(jnp.float32)
    back_preact = (back_message * silu_slope(preact)).astype(jnp.bfloat16)
    grad_msg = contract(row_block, back_preact) / cell_rows
    back_pulled = matmul(back_preact, w_msg.T).astype(jnp.bfloat16).reshape(pulled.shape)
    returned = route_dec(back_pulled[::-1, ::-1])[::-1, ::-1]
    back_node = jax.ops.segment_sum(
        returned.reshape(-1, features).astype(jnp.float32),
        dec_node[0].reshape(-1),
        num_segments=node_rows,
    )
    back_state, grad_up, grad_down = node_backward(
        back_node, node_state, node_gain, w_up, w_down, inv_rms, normed, activation, hidden
    )
    back_state_half = back_state.astype(jnp.bfloat16)
    toward = back_state_half[enc_node[0]]
    came_back = route_enc(toward[::-1, ::-1])[::-1, ::-1]
    weighted_back = (edge_scale[..., None] * came_back.astype(jnp.float32)).reshape(-1, features)
    back_proj = jax.ops.segment_sum(
        weighted_back, send_cells.reshape(-1), num_segments=cell_rows
    ).astype(jnp.bfloat16)
    grad_enc = contract(grid_latent, back_proj) / cell_rows
    grid_grad = back_blend + matmul(back_proj, w_enc.T)
    partials = (grad_enc, grad_up / cell_rows, grad_down / cell_rows, grad_msg, grad_dec, grad_out)
    shares = side_by_side(
        (
            partials[0].astype(jnp.bfloat16),
            partials[1].astype(jnp.bfloat16),
            partials[2].astype(jnp.bfloat16),
            partials[3].astype(jnp.bfloat16),
            partials[4].astype(jnp.bfloat16),
            partials[5].astype(jnp.bfloat16),
        ),
        (("lat", "lon", "mesh_0"), "mesh_1"),
        0,
        1,
    )
    return (grid_grad,) + tuple(shares)


def solution(mesh):
    torus = Mesh(
        mesh.devices.reshape(mesh.shape["lat"], mesh.shape["lon"], 4, 2),
        ("lat", "lon", "mesh_0", "mesh_1"),
    )
    in_specs = (
        P(LAT_LON_MESH, None),
        P(LAT_LON_MESH, None),
        P(LAT_LON_MESH),
        P(LAT_LON_MESH, None),
        P(),
        P(),
        P(),
        P(),
        P(),
        P(),
        P(),
        P(LAT_LON_MESH, None, None, None, None),
        P(LAT_LON_MESH, None, None, None),
        P(LAT_LON_MESH, None, None, None, None),
        P(LAT_LON_MESH, None, None, None, None),
        P(LAT_LON_MESH, None, None, None, None),
        P(LAT_LON_MESH, None, None, None, None),
        P(LAT_LON_MESH, None, None, None, None),
    )
    out_specs = (
        P(LAT_LON_MESH, None),
        P(LAT_LON_MESH, None),
        P(LAT_LON_MESH, None),
        P(LAT_LON_MESH, None),
        P(LAT_LON_MESH, None),
        P(LAT_LON_MESH, None),
        P(LAT_LON_MESH, None),
    )
    return jax.shard_map(
        on_device, mesh=torus, in_specs=in_specs, out_specs=out_specs, check_vma=False
    )
```

profile of v0, /device:TPU:1, one launch (start us, length us, event | category | flops | bytes accessed | tf_op | source)
XLA Modules:
  0.0 537.3 jit_solution(137742396021707262)
XLA Ops:
  5.3 5.4 %gather_fusion = bf16[1512,512]{1,0:T(8,128)(2,1)} fusion(bf16[1024,512]{1,0:T(8,128)(2,1)S(1)} %convolution_convert_fusion.2, s32[2048]{0:T(1024)S(1)} %get-tuple-element.35), kind=kCustom, calls=%fused_computation | custom fusion | bytes 3102624 | tf_op jit(solution)/shard_map/gather | solution.py:147
  17.1 28.3 %all_to_all.30 = bf16[3,3,8,21,512]{4,3,1,0,2:T(8,128)(2,1)S(1)} all-to-all(bf16[3,3,8,21,512]{4,3,1,0,2:T(8,128)(2,1)S(1)} %copy.142), channel_id=1, replica_groups=mesh['lat'=4,'lon'=4,'mesh_0'=4,'mesh_1'=2] {'mesh_0','mesh_1'}, dimensions={2} | all-to-all | bytes 3096576 | tf_op jit(solution)/shard_map/all_to_all | solution.py:95
  48.7 10.7 %collective-permute-done = bf16[1,3,8,21,512]{4,2,3,1,0:T(8,128)(2,1)S(1)} collective-permute-done((bf16[1,3,8,21,512]{4,2,3,1,0:T(8,128)(2,1)S(1)}, bf16[1,3,8,21,512]{4,2,3,1,0:T(8,128)(2,1)S(1)}, u32[]{:S(2)}, u32[]{:S(2)}) %collective-permute-start) | collective-permute-done | bytes 516128 | tf_op jit(solution)/shard_map/ppermute | solution.py:18
  66.7 16.7 %collective-permute-done.2 = bf16[5,1,8,21,512]{4,2,3,1,0:T(8,128)(2,1)} collective-permute-done((bf16[5,1,8,21,512]{4,2,3,1,0:T(8,128)(2,1)S(1)}, bf16[5,1,8,21,512]{4,2,3,1,0:T(8,128)(2,1)}, u32[]{:S(2)}, u32[]{:S(2)}) %collective-permute-start.2) | collective-permute-done | bytes 860192 | tf_op jit(solution)/shard_map/ppermute | solution.py:18
  94.7 10.9 %scatter_fusion = f32[320,512]{1,0:T(8,128)S(1)} fusion(f32[320,512]{1,0:T(8,128)S(1)} %convert_element_type.105, s32[1512]{0:T(1024)S(1)} %reshape.235, f32[1512,512]{1,0:T(8,128)} %reshape.237), kind=kCustom, calls=%fused_computation.4 | custom fusion | flops 774144 | bytes 9295776 | tf_op jit(solution)/shard_map/scatter-add | solution.py:151
  107.9 7.5 %gather_fusion.1 = bf16[2304,512]{1,0:T(8,128)(2,1)} fusion(bf16[320,512]{1,0:T(8,128)(2,1)S(1)} %fusion.16, s32[3072]{0:T(1024)S(1)} %get-tuple-element.33), kind=kCustom, calls=%fused_computation.1 | custom fusion | bytes 4727808 | tf_op jit(solution)/shard_map/gather | solution.py:159
  117.3 33.7 %all_to_all.31 = bf16[3,3,8,32,512]{4,3,1,0,2:T(8,128)(2,1)S(1)} all-to-all(bf16[3,3,8,32,512]{4,3,1,0,2:T(8,128)(2,1)S(1)} %copy.147), channel_id=1, replica_groups=mesh['lat'=4,'lon'=4,'mesh_0'=4,'mesh_1'=2] {'mesh_0','mesh_1'}, dimensions={2} | all-to-all | bytes 4718592 | tf_op jit(solution)/shard_map/all_to_all | solution.py:102
  154.1 16.4 %collective-permute-done.4 = bf16[1,3,8,32,512]{4,3,2,1,0:T(8,128)(2,1)S(1)} collective-permute-done((bf16[1,3,8,32,512]{4,3,2,1,0:T(8,128)(2,1)S(1)}, bf16[1,3,8,32,512]{4,3,2,1,0:T(8,128)(2,1)S(1)}, u32[]{:S(2)}, u32[]{:S(2)}) %collective-permute-start.4) | collective-permute-done | bytes 786464 | tf_op jit(solution)/shard_map/ppermute | solution.py:18
  178.9 25.7 %collective-permute-done.6 = bf16[5,1,8,32,512]{4,3,2,1,0:T(8,128)(2,1)S(1)} collective-permute-done((bf16[5,1,8,32,512]{4,3,2,1,0:T(8,128)(2,1)}, bf16[5,1,8,32,512]{4,3,2,1,0:T(8,128)(2,1)S(1)}, u32[]{:S(2)}, u32[]{:S(2)}) %collective-permute-start.6) | collective-permute-done | bytes 1310752 | tf_op jit(solution)/shard_map/ppermute | solution.py:18
  216.3 19.1 %scatter_custom_fusion.1 = f32[1024,512]{1,0:T(8,128)S(1)} fusion(s32[2304]{0:T(1024)} %reshape.243, f32[2304,512]{1,0:T(8,128)} %fusion.47, f32[]{:T(128)} %constant.46.clone.1, f32[2304]{0:T(1024)} %broadcast_select_fusion, f32[]{:T(128)} %constant.14.clone.1), kind=kCustom, calls=%fused_computation.12 | custom fusion | flops 7077888 | bytes 6829056 | tf_op jit(solution)/shard_map/scatter-add | solution.py:166
  243.0 7.5 %gather_fusion.2 = bf16[2304,512]{1,0:T(8,128)(2,1)} fusion(bf16[1024,512]{1,0:T(8,128)(2,1)S(1)} %convolution_convert_fusion.1, s32[3072]{0:T(1024)S(1)} %copy-done.42), kind=kCustom, calls=%fused_computation.2 | custom fusion | bytes 4727808 | tf_op jit(solution)/shard_map/gather | solution.py:176
  257.9 35.2 %all_to_all.32 = bf16[3,3,8,32,512]{4,3,1,0,2:T(8,128)(2,1)S(1)} all-to-all(bf16[3,3,8,32,512]{4,3,1,0,2:T(8,128)(2,1)} %rev.18), channel_id=1, replica_groups=mesh['lat'=4,'lon'=4,'mesh_0'=4,'mesh_1'=2] {'mesh_0','mesh_1'}, dimensions={2} | all-to-all | bytes 4718592 | tf_op jit(solution)/shard_map/all_to_all | solution.py:102
  296.0 16.6 %collective-permute-done.8 = bf16[1,3,8,32,512]{4,3,1,0,2:T(8,128)(2,1)S(1)} collective-permute-done((bf16[1,3,8,32,512]{4,3,1,0,2:T(8,128)(2,1)S(1)}, bf16[1,3,8,32,512]{4,3,1,0,2:T(8,128)(2,1)S(1)}, u32[]{:S(2)}, u32[]{:S(2)}) %collective-permute-start.8) | collective-permute-done | bytes 786464 | tf_op jit(solution)/shard_map/ppermute | solution.py:18
  319.7 27.0 %collective-permute-done.10 = bf16[5,1,8,32,512]{4,3,1,0,2:T(8,128)(2,1)S(1)} collective-permute-done((bf16[5,1,8,32,512]{4,3,1,0,2:T(8,128)(2,1)}, bf16[5,1,8,32,512]{4,3,1,0,2:T(8,128)(2,1)S(1)}, u32[]{:S(2)}, u32[]{:S(2)}) %collective-permute-start.10) | collective-permute-done | bytes 1310752 | tf_op jit(solution)/shard_map/ppermute | solution.py:18
  353.9 16.4 %scatter_custom_fusion.2 = f32[320,512]{1,0:T(8,128)S(1)} fusion(s32[2304]{0:T(1024)S(1)} %reshape.251, f32[2304,512]{1,0:T(8,128)} %bitcast.74, f32[]{:T(128)} %constant.14.clone.1), kind=kCustom, calls=%fused_computation.75 | custom fusion | flops 1179648 | bytes 655872 | tf_op jit(solution)/shard_map/scatter-add | solution.py:181
  380.6 28.1 %all_to_all.33 = bf16[3,3,8,21,512]{4,3,1,0,2:T(8,128)(2,1)S(1)} all-to-all(bf16[3,3,8,21,512]{4,3,1,0,2:T(8,128)(2,1)S(1)} %copy.153), channel_id=1, replica_groups=mesh['lat'=4,'lon'=4,'mesh_0'=4,'mesh_1'=2] {'mesh_0','mesh_1'}, dimensions={2} | all-to-all | bytes 3096576 | tf_op jit(solution)/shard_map/all_to_all | solution.py:95
  411.9 10.7 %collective-permute-done.12 = bf16[1,3,8,21,512]{4,2,3,1,0:T(8,128)(2,1)S(1)} collective-permute-done((bf16[1,3,8,21,512]{4,2,3,1,0:T(8,128)(2,1)S(1)}, bf16[1,3,8,21,512]{4,2,3,1,0:T(8,128)(2,1)S(1)}, u32[]{:S(2)}, u32[]{:S(2)}) %collective-permute-start.12) | collective-permute-done | bytes 516128 | tf_op jit(solution)/shard_map/ppermute | solution.py:18
  429.1 16.0 %collective-permute-done.14 = bf16[5,1,8,21,512]{4,2,3,1,0:T(8,128)(2,1)S(1)} collective-permute-done((bf16[5,1,8,21,512]{4,2,3,1,0:T(8,128)(2,1)S(1)}, bf16[5,1,8,21,512]{4,2,3,1,0:T(8,128)(2,1)S(1)}, u32[]{:S(2)}, u32[]{:S(2)}) %collective-permute-start.14) | collective-permute-done | bytes 860192 | tf_op jit(solution)/shard_map/ppermute | solution.py:18
  455.3 10.7 %scatter_custom_fusion.3 = f32[1024,512]{1,0:T(8,128)S(1)} fusion(s32[1512]{0:T(1024)S(1)} %reshape.259, f32[1512,512]{1,0:T(8,128)} %reshape.261, f32[]{:T(128)} %constant.14.clone.1), kind=kCustom, calls=%fused_computation.58 | custom fusion | flops 774144 | bytes 2097664 | tf_op jit(solution)/shard_map/scatter-add | solution.py:193
  481.7 5.6 %reshape_reshape.3 = bf16[64,2,4,2644]{3,2,1,0:T(4,128)(2,1)} reshape(bf16[512,2644]{1,0:T(8,128)(2,1)} %copy.164) | data formatting | bytes 5414912 | tf_op jit(solution)/shard_map/reshape;reshape | solution.py:29
  490.0 9.7 %all_to_all.34 = bf16[2,64,4,2644]{3,2,1,0:T(4,128)(2,1)} all-to-all(bf16[2,64,4,2644]{3,2,1,0:T(4,128)(2,1)S(1)} %copy.165), channel_id=1, replica_groups=mesh['lat'=4,'lon'=4,'mesh_0'=4,'mesh_1'=2] {'mesh_1'}, dimensions={0} | all-to-all | bytes 5414912 | tf_op jit(solution)/shard_map/all_to_all | solution.py:35
  499.7 5.1 reduce_sum.41
  504.9 7.9 %all-to-all-start.5 = ((bf16[64,4,2644]{2,1,0:T(4,128)(2,1)}), bf16[64,4,2644]{2,1,0:T(4,128)(2,1)}, u32[]{:S(2)}, u32[]{:S(2)}) async-start(bf16[64,4,2644]{2,1,0:T(4,128)(2,1)} %reduce_sum.41), calls=%async_computation.5 | async-start | bytes 2752512 | tf_op jit(solution)/shard_map/all_to_all | solution.py:43
  516.5 17.6 %all-to-all-done.5 = bf16[64,4,2644]{2,1,0:T(4,128)(2,1)} async-done(((bf16[64,4,2644]{2,1,0:T(4,128)(2,1)}), bf16[64,4,2644]{2,1,0:T(4,128)(2,1)}, u32[]{:S(2)}, u32[]{:S(2)}) %all-to-all-start.5) | async-done | bytes 1353760 | tf_op jit(solution)/shard_map/all_to_all | solution.py:43
  (228 shorter events, 146.6 us)
Async XLA Ops:
  0.6 212.1 %copy-start = (bf16[512,512]{1,0:T(8,128)(2,1)S(1)}, bf16[512,512]{1,0:T(8,128)(2,1)}, u32[]{:S(2)}) copy-start(bf16[512,512]{1,0:T(8,128)(2,1)} %param.26) | copy-start | bytes 1572868
  45.7 13.8 %collective-permute-start = (bf16[1,3,8,21,512]{4,2,3,1,0:T(8,128)(2,1)S(1)}, bf16[1,3,8,21,512]{4,2,3,1,0:T(8,128)(2,1)S(1)}, u32[]{:S(2)}, u32[]{:S(2)}) collective-permute-start(bf16[1,3,8,21,512]{4,2,3,1,0:T(8,128)(2,1)S(1)} %copy.143), channel_id=1, source_target_pairs={{0,32},{32,64},{64,96},{96,0},{1,33},{33,65},{65,97},{97,1},{2,34}... | collective-permute-start | bytes 1548296 | tf_op jit(solution)/shard_map/ppermute | solution.py:18
  47.2 12.9 %collective-permute-start.1 = (bf16[1,3,8,21,512]{4,2,3,1,0:T(8,128)(2,1)S(1)}, bf16[1,3,8,21,512]{4,2,3,1,0:T(8,128)(2,1)S(1)}, u32[]{:S(2)}, u32[]{:S(2)}) collective-permute-start(bf16[1,3,8,21,512]{4,2,3,1,0:T(8,128)(2,1)S(1)} %copy.144), channel_id=1, source_target_pairs={{32,0},{64,32},{96,64},{0,96},{33,1},{65,33},{97,65},{1,97},{34,2}... | collective-permute-start | bytes 1548296 | tf_op jit(solution)/shard_map/ppermute | solution.py:20
  61.8 21.7 %collective-permute-start.2 = (bf16[5,1,8,21,512]{4,2,3,1,0:T(8,128)(2,1)S(1)}, bf16[5,1,8,21,512]{4,2,3,1,0:T(8,128)(2,1)}, u32[]{:S(2)}, u32[]{:S(2)}) collective-permute-start(bf16[5,1,8,21,512]{4,2,3,1,0:T(8,128)(2,1)S(1)} %get-tuple-element.13), channel_id=1, source_target_pairs={{0,8},{8,16},{16,24},{24,0},{1,9},{9,17},{17,25},{25,1},{2,10},{10... | collective-permute-start | bytes 2580488 | tf_op jit(solution)/shard_map/ppermute | solution.py:18
  63.5 20.0 %collective-permute-start.3 = (bf16[5,1,8,21,512]{4,2,3,1,0:T(8,128)(2,1)S(1)}, bf16[5,1,8,21,512]{4,2,3,1,0:T(8,128)(2,1)}, u32[]{:S(2)}, u32[]{:S(2)}) collective-permute-start(bf16[5,1,8,21,512]{4,2,3,1,0:T(8,128)(2,1)S(1)} %get-tuple-element.14), channel_id=1, source_target_pairs={{8,0},{16,8},{24,16},{0,24},{9,1},{17,9},{25,17},{1,25},{10,2},{18... | collective-permute-start | bytes 2580488 | tf_op jit(solution)/shard_map/ppermute | solution.py:20
  151.2 19.3 %collective-permute-start.4 = (bf16[1,3,8,32,512]{4,3,2,1,0:T(8,128)(2,1)S(1)}, bf16[1,3,8,32,512]{4,3,2,1,0:T(8,128)(2,1)S(1)}, u32[]{:S(2)}, u32[]{:S(2)}) collective-permute-start(bf16[1,3,8,32,512]{4,3,2,1,0:T(8,128)(2,1)S(1)} %copy.175), channel_id=1, source_target_pairs={{0,32},{32,64},{64,96},{96,0},{1,33},{33,65},{65,97},{97,1},{2,34}... | collective-permute-start | bytes 2359304 | tf_op jit(solution)/shard_map/ppermute | solution.py:18
  151.9 19.0 %collective-permute-start.5 = (bf16[1,3,8,32,512]{4,3,2,1,0:T(8,128)(2,1)S(1)}, bf16[1,3,8,32,512]{4,3,2,1,0:T(8,128)(2,1)S(1)}, u32[]{:S(2)}, u32[]{:S(2)}) collective-permute-start(bf16[1,3,8,32,512]{4,3,2,1,0:T(8,128)(2,1)S(1)} %copy.176), channel_id=1, source_target_pairs={{32,0},{64,32},{96,64},{0,96},{33,1},{65,33},{97,65},{1,97},{34,2}... | collective-permute-start | bytes 2359304 | tf_op jit(solution)/shard_map/ppermute | solution.py:20
  174.7 30.0 %collective-permute-start.6 = (bf16[5,1,8,32,512]{4,3,2,1,0:T(8,128)(2,1)}, bf16[5,1,8,32,512]{4,3,2,1,0:T(8,128)(2,1)S(1)}, u32[]{:S(2)}, u32[]{:S(2)}) collective-permute-start(bf16[5,1,8,32,512]{4,3,2,1,0:T(8,128)(2,1)} %get-tuple-element.9), channel_id=1, source_target_pairs={{0,8},{8,16},{16,24},{24,0},{1,9},{9,17},{17,25},{25,1},{2,10},{10... | collective-permute-start | bytes 3932168 | tf_op jit(solution)/shard_map/ppermute | solution.py:18
  175.6 29.0 %collective-permute-start.7 = (bf16[5,1,8,32,512]{4,3,2,1,0:T(8,128)(2,1)}, bf16[5,1,8,32,512]{4,3,2,1,0:T(8,128)(2,1)}, u32[]{:S(2)}, u32[]{:S(2)}) collective-permute-start(bf16[5,1,8,32,512]{4,3,2,1,0:T(8,128)(2,1)} %get-tuple-element.10), channel_id=1, source_target_pairs={{8,0},{16,8},{24,16},{0,24},{9,1},{17,9},{25,17},{1,25},{10,2},{18... | collective-permute-start | bytes 3932168 | tf_op jit(solution)/shard_map/ppermute | solution.py:20
  293.3 19.3 %collective-permute-start.8 = (bf16[1,3,8,32,512]{4,3,1,0,2:T(8,128)(2,1)S(1)}, bf16[1,3,8,32,512]{4,3,1,0,2:T(8,128)(2,1)S(1)}, u32[]{:S(2)}, u32[]{:S(2)}) collective-permute-start(bf16[1,3,8,32,512]{4,3,1,0,2:T(8,128)(2,1)S(1)} %get-tuple-element.16), channel_id=1, source_target_pairs={{0,32},{32,64},{64,96},{96,0},{1,33},{33,65},{65,97},{97,1},{2,34}... | collective-permute-start | bytes 2359304 | tf_op jit(solution)/shard_map/ppermute | solution.py:18
  293.4 19.6 %collective-permute-start.9 = (bf16[1,3,8,32,512]{4,3,1,0,2:T(8,128)(2,1)S(1)}, bf16[1,3,8,32,512]{4,3,1,0,2:T(8,128)(2,1)S(1)}, u32[]{:S(2)}, u32[]{:S(2)}) collective-permute-start(bf16[1,3,8,32,512]{4,3,1,0,2:T(8,128)(2,1)S(1)} %get-tuple-element.15), channel_id=1, source_target_pairs={{32,0},{64,32},{96,64},{0,96},{33,1},{65,33},{97,65},{1,97},{34,2}... | collective-permute-start | bytes 2359304 | tf_op jit(solution)/shard_map/ppermute | solution.py:20
  316.7 30.0 %collective-permute-start.10 = (bf16[5,1,8,32,512]{4,3,1,0,2:T(8,128)(2,1)}, bf16[5,1,8,32,512]{4,3,1,0,2:T(8,128)(2,1)S(1)}, u32[]{:S(2)}, u32[]{:S(2)}) collective-permute-start(bf16[5,1,8,32,512]{4,3,1,0,2:T(8,128)(2,1)} %get-tuple-element.7), channel_id=1, source_target_pairs={{0,8},{8,16},{16,24},{24,0},{1,9},{9,17},{17,25},{25,1},{2,10},{10... | collective-permute-start | bytes 3932168 | tf_op jit(solution)/shard_map/ppermute | solution.py:18
  317.8 28.9 %collective-permute-start.11 = (bf16[5,1,8,32,512]{4,3,1,0,2:T(8,128)(2,1)}, bf16[5,1,8,32,512]{4,3,1,0,2:T(8,128)(2,1)}, u32[]{:S(2)}, u32[]{:S(2)}) collective-permute-start(bf16[5,1,8,32,512]{4,3,1,0,2:T(8,128)(2,1)} %get-tuple-element.8), channel_id=1, source_target_pairs={{8,0},{16,8},{24,16},{0,24},{9,1},{17,9},{25,17},{1,25},{10,2},{18... | collective-permute-start | bytes 3932168 | tf_op jit(solution)/shard_map/ppermute | solution.py:20
  350.7 19.6 %copy-start.26 = (f32[320,512]{1,0:T(8,128)S(1)}, f32[320,512]{1,0:T(8,128)}, u32[]{:S(2)}) copy-start(f32[320,512]{1,0:T(8,128)} %copy-done.25) | copy-start | bytes 1966084
  350.7 19.6 %copy-start.49 = (bf16[512,512]{1,0:T(8,128)(2,1)S(1)}, bf16[512,512]{1,0:T(8,128)(2,1)}, u32[]{:S(2)}) copy-start(bf16[512,512]{1,0:T(8,128)(2,1)} %param.25) | copy-start | bytes 1572868
  353.9 17.0 %copy-start.22 = (bf16[512,512]{1,0:T(8,128)(2,1)S(1)}, bf16[512,512]{1,0:T(8,128)(2,1)}, u32[]{:S(2)}) copy-start(bf16[512,512]{1,0:T(8,128)(2,1)} %param.24) | copy-start | bytes 1572868
  409.0 13.6 %collective-permute-start.12 = (bf16[1,3,8,21,512]{4,2,3,1,0:T(8,128)(2,1)S(1)}, bf16[1,3,8,21,512]{4,2,3,1,0:T(8,128)(2,1)S(1)}, u32[]{:S(2)}, u32[]{:S(2)}) collective-permute-start(bf16[1,3,8,21,512]{4,2,3,1,0:T(8,128)(2,1)S(1)} %copy.154), channel_id=1, source_target_pairs={{0,32},{32,64},{64,96},{96,0},{1,33},{33,65},{65,97},{97,1},{2,34}... | collective-permute-start | bytes 1548296 | tf_op jit(solution)/shard_map/ppermute | solution.py:18
  409.2 13.7 %collective-permute-start.13 = (bf16[1,3,8,21,512]{4,2,3,1,0:T(8,128)(2,1)S(1)}, bf16[1,3,8,21,512]{4,2,3,1,0:T(8,128)(2,1)S(1)}, u32[]{:S(2)}, u32[]{:S(2)}) collective-permute-start(bf16[1,3,8,21,512]{4,2,3,1,0:T(8,128)(2,1)S(1)} %copy.155), channel_id=1, source_target_pairs={{32,0},{64,32},{96,64},{0,96},{33,1},{65,33},{97,65},{1,97},{34,2}... | collective-permute-start | bytes 1548296 | tf_op jit(solution)/shard_map/ppermute | solution.py:20
  424.7 20.4 %collective-permute-start.14 = (bf16[5,1,8,21,512]{4,2,3,1,0:T(8,128)(2,1)S(1)}, bf16[5,1,8,21,512]{4,2,3,1,0:T(8,128)(2,1)S(1)}, u32[]{:S(2)}, u32[]{:S(2)}) collective-permute-start(bf16[5,1,8,21,512]{4,2,3,1,0:T(8,128)(2,1)S(1)} %copy.159), channel_id=1, source_target_pairs={{0,8},{8,16},{16,24},{24,0},{1,9},{9,17},{17,25},{25,1},{2,10},{10... | collective-permute-start | bytes 2580488 | tf_op jit(solution)/shard_map/ppermute | solution.py:18
  427.2 19.1 %collective-permute-start.15 = (bf16[5,1,8,21,512]{4,2,3,1,0:T(8,128)(2,1)}, bf16[5,1,8,21,512]{4,2,3,1,0:T(8,128)(2,1)}, u32[]{:S(2)}, u32[]{:S(2)}) collective-permute-start(bf16[5,1,8,21,512]{4,2,3,1,0:T(8,128)(2,1)} %copy.160), channel_id=1, source_target_pairs={{8,0},{16,8},{24,16},{0,24},{9,1},{17,9},{25,17},{1,25},{10,2},{18... | collective-permute-start | bytes 2580488 | tf_op jit(solution)/shard_map/ppermute | solution.py:20
  429.1 18.6 %copy-start.11 = (bf16[5,3,8,21,512]{4,3,2,1,0:T(8,128)(2,1)S(1)}, bf16[5,3,8,21,512]{4,3,2,1,0:T(8,128)(2,1)}, u32[]{:S(2)}) copy-start(bf16[5,3,8,21,512]{4,3,2,1,0:T(8,128)(2,1)} %copy-done.10) | copy-start | bytes 7741444
  455.3 14.3 %copy-start.34 = (bf16[320,512]{1,0:T(8,128)(2,1)S(1)}, bf16[320,512]{1,0:T(8,128)(2,1)}, u32[]{:S(2)}) copy-start(bf16[320,512]{1,0:T(8,128)(2,1)} %copy-done.33) | copy-start | bytes 983044
  504.9 29.3 %all-to-all-start.5 = ((bf16[64,4,2644]{2,1,0:T(4,128)(2,1)}), bf16[64,4,2644]{2,1,0:T(4,128)(2,1)}, u32[]{:S(2)}, u32[]{:S(2)}) async-start(bf16[64,4,2644]{2,1,0:T(4,128)(2,1)} %reduce_sum.41), calls=%async_computation.5 | async-start | bytes 2752512 | tf_op jit(solution)/shard_map/all_to_all | solution.py:43
  512.8 24.1 %copy-start.1 = (bf16[512,512]{1,0:T(8,128)(2,1)S(1)}, bf16[512,512]{1,0:T(8,128)(2,1)}, u32[]{:S(2)}) copy-start(bf16[512,512]{1,0:T(8,128)(2,1)} %param.26) | copy-start | bytes 1572868
  (43 other events, 168.7 us)
where the time goes:
time: 547 us; the launch traced here: 537 us
  waiting for transfers between devices  158 us (29%)
  blocking collectives  135 us (25%)
  local copies, waits for them, and re-layouts  95.1 us (17%)
  other arithmetic  87 us (16%)
  starting transfers between devices  31.8 us (6%)
  matrix products  28.1 us (5%)
    ppermute x8, waiting for transfers between devices, extended_2(): lax.ppermute(tail, axis, [(i, (i + 1) % count) for i in range(count)])  140 us
    all_to_all x2, blocking collectives, route_dec(): lax.all_to_all(bucket, MESH, split_axis=2, concat_axis=2, tiled=True)  68.9 us
    all_to_all x2, blocking collectives, route_enc(): lax.all_to_all(bucket, MESH, split_axis=2, concat_axis=2, tiled=True)  56.4 us
    scatter-add x1, other arithmetic, on_device(): jax.ops.segment_sum(weighted, cell_ids, num_segments=cell_rows)  19.1 us
    all_to_all x1, waiting for transfers between devices, sum_in_two_steps(): lax.all_to_all(nearer.astype(jnp.bfloat16), far, split_axis=0, concat_axi...  17.6 us
    dot_general x12, matrix products, matmul(): return jnp.dot(left, right, preferred_element_type=jnp.float32)  17 us
    ppermute x8, starting transfers between devices, extended_2(): lax.ppermute(head, axis, [((i + 1) % count, i) for i in range(count)])  16.6 us
    scatter-add x1, other arithmetic, on_device(): jax.ops.segment_sum(returned.reshape(-1, features).astype(jnp.float32), d...  16.4 us
  transfers between devices with their start and end apart: 17, of which 10 were waited for; matrix products, arithmetic and copies ran while one was open for 2% of the time, Pallas kernels for 0%

commit v1 on v0

v1 whole, which is shorter than its diff:
```python
import jax
import jax.numpy as jnp
from jax import lax
from jax.experimental import pallas as pl
from jax.experimental.pallas import tpu as pltpu
from jax.sharding import PartitionSpec as P

AXES = ("lat", "lon", "mesh")
MESH_ID = pl.DeviceIdType.MESH
W = 512
CELLS = 1024
NODES = 320
SE = 21
SEP = 24
SD = 32
EROWS = 8 * SEP
DROWS = 8 * SD
T_ENC_CELL, T_ENC_NODE, T_DEC_NODE, T_DEC_CELL, T_ENC_SCALE, T_DEC_SCALE, T_AREA = (
    0,
    9,
    18,
    27,
    36,
    45,
    54,
)
VMEM_LIMIT = 67043328
BF = jnp.bfloat16
F32 = jnp.float32


def dot(a, b):
    return jnp.dot(a, b, preferred_element_type=F32)


def dot_nt(a, b):
    return lax.dot_general(a, b, (((1,), (1,)), ((), ())), preferred_element_type=F32)


def dot_tn(a, b):
    return lax.dot_general(a, b, (((0,), (0,)), ((), ())), preferred_element_type=F32)


def sigmoid(x):
    return 0.5 * jnp.tanh(0.5 * x) + 0.5


def slope(x):
    s = sigmoid(x)
    return s * (1.0 + x * (1.0 - s))


def kernel(
    enc_cell_in,
    enc_node_in,
    dec_node_in,
    dec_cell_in,
    enc_weight_in,
    dec_weight_in,
    enc_live_in,
    area_in,
    target_t_in,
    w_out_t_in,
    node_gain_in,
    grid_latent_in,
    mesh_latent_in,
    w_enc_in,
    w_up_in,
    w_down_in,
    w_msg_in,
    w_dec_in,
    grid_grad,
    g_enc,
    g_up,
    g_down,
    g_msg,
    g_dec,
    g_out,
    enc_cell,
    enc_node,
    dec_node,
    dec_cell,
    enc_weight,
    dec_weight,
    enc_live,
    area,
    target_t,
    w_out_t,
    node_gain,
    grid_latent,
    mesh_latent,
    w_enc,
    w_up,
    w_down,
    w_msg,
    w_dec,
    target,
    pad,
    table,
    cols,
    es,
    ed,
    ds_,
    dd,
    bs,
    bd,
    fs,
    fd,
    acc_n,
    acc_c,
    gath,
    blend,
    bhalf,
    bgath,
    resid,
    wo,
    nstate,
    act,
    normed,
    hidden,
    nhalf,
    prew,
    aggb,
    ga,
    la_c,
    ha,
    la_y,
    ha2,
    la_z,
    gb,
    lb_c,
    hu,
    lu_y,
    hu2,
    lu_z,
    hv,
    lv_z,
    hv2,
    lv_y,
    hm,
    lm,
    ssem,
    rsem,
    gs,
    gr,
    ls,
):
    la, lo, me = lax.axis_index("lat"), lax.axis_index("lon"), lax.axis_index("mesh")
    core = lax.rem(me, 2)

    def device(dla, dlo, part):
        return {"lat": lax.rem(la + dla, 4), "lon": lax.rem(lo + dlo, 4), "mesh": part}

    barrier = pltpu.get_barrier_semaphore()
    peers = 0
    for p in range(3):
        for q in range(3):
            for d in range(8):
                if p == 1 and q == 1 and d == 0:
                    continue
                pl.semaphore_signal(
                    barrier,
                    inc=1,
                    device_id=device(p + 3, q + 3, lax.rem(me + d, 8)),
                    device_id_type=MESH_ID,
                )
                peers += 1
    for dla, dlo in ((2, 0), (0, 2)):
        pl.semaphore_signal(
            barrier, inc=1, device_id=device(dla, dlo, me), device_id_type=MESH_ID
        )
        peers += 1

    loads = []
    for i, (src, dst) in enumerate(
        (
            (enc_cell_in, enc_cell),
            (enc_node_in, enc_node),
            (dec_node_in, dec_node),
            (dec_cell_in, dec_cell),
            (enc_weight_in, enc_weight),
            (dec_weight_in, dec_weight),
            (enc_live_in, enc_live),
            (area_in, area),
            (target_t_in, target_t),
            (w_out_t_in, w_out_t),
            (node_gain_in, node_gain),
            (grid_latent_in, grid_latent),
            (mesh_latent_in, mesh_latent),
            (w_enc_in, w_enc),
            (w_up_in, w_up),
            (w_down_in, w_down),
            (w_msg_in, w_msg),
            (w_dec_in, w_dec),
        )
    ):
        loads.append(pltpu.make_async_copy(src, dst, ls.at[i]))
        loads[i].start()

    for copy in loads[:11]:
        copy.wait()

    table[...] = jnp.zeros_like(table)
    pad[...] = jnp.zeros_like(pad)

    def fill(k, carry):
        def put(block, value, slots, stride):
            pad[:, 0:slots] = value
            row = pad[0:1, :]
            for m in range(1, 8):
                row = row + pltpu.roll(pad[m : m + 1, :], m * stride, axis=1)
            table[pl.ds(block + k, 1), :] = row

        put(T_DEC_NODE, dec_node[k].astype(F32), SD, SD)
        put(T_DEC_CELL, dec_cell[k].astype(F32), SD, SD)
        put(T_DEC_SCALE, dec_weight[k], SD, SD)
        pad[...] = jnp.zeros_like(pad)
        put(T_ENC_CELL, enc_cell[k].astype(F32), SE, SEP)
        put(T_ENC_NODE, enc_node[k].astype(F32), SE, SEP)
        here = lax.broadcasted_iota(jnp.int32, (8, 8), 0) == lax.broadcasted_iota(
            jnp.int32, (8, 8), 1
        )
        live = jnp.sum(jnp.where(here, enc_live[k].astype(F32), 0.0), axis=1, keepdims=True)
        slot = lax.broadcasted_iota(jnp.int32, (8, SE), 1).astype(F32)
        put(T_ENC_SCALE, jnp.where(slot < live, enc_weight[k], 0.0), SE, SEP)
        return carry

    lax.fori_loop(0, 9, fill, 0)
    for b in range(4):
        table[T_AREA + b : T_AREA + b + 1, 0:128] = area[2 * b : 2 * b + 1, :]
        table[T_AREA + b : T_AREA + b + 1, 128:256] = area[2 * b + 1 : 2 * b + 2, :]
    cols[...] = table[...].T
    wo[...] = jnp.zeros_like(wo)
    wo[0:84, :] = w_out_t[...]
    target[...] = jnp.zeros_like(target)
    target[0:84, :] = target_t[...].astype(F32)
    loads[11].wait()

    def column(block, k, rows):
        turned = pltpu.roll(cols[...], lax.rem(128 - (block + k), 128), axis=1)
        return turned[0:rows, 0:1]

    def pick(block, k, rows, width):
        index = column(block, k, rows).astype(jnp.int32)
        return (index == lax.broadcasted_iota(jnp.int32, (rows, width), 1)).astype(F32).astype(BF)

    def place(block, k, rows, width):
        index = table[pl.ds(block + k, 1), :][:, 0:width].astype(jnp.int32)
        return (index == lax.broadcasted_iota(jnp.int32, (rows, width), 0)).astype(F32)

    def chunk_of(t):
        return lax.rem(4 * t + 8, 9)

    def valid(k, sign):
        at = la + sign * (k // 3 - 1)
        return (at >= 0) & (at < 4)

    def send(phase, k, src, dst, sign):
        dla = k // 3 - 1
        dlo = lax.rem(k, 3) - 1
        for d in (4, 3, 5, 2, 6, 1, 7, 0):
            part = lax.rem(me + d, 8)
            copy = pltpu.make_async_remote_copy(
                src_ref=src.at[k * 8 + part],
                dst_ref=dst.at[k * 8 + me],
                send_sem=ssem.at[phase, k],
                recv_sem=rsem.at[phase, k],
                device_id=device(sign * dla + 4, sign * dlo + 4, part),
                device_id_type=MESH_ID,
            )
            if d == 0:
                pl.when(k != 4)(copy.start)
            else:
                copy.start()

    def await_bytes(sem, phase, k, buf):
        whole = buf.at[pl.ds(k * 8, 8)]
        most = buf.at[pl.ds(k * 8, 7)]

        @pl.when(k != 4)
        def _():
            pltpu.make_async_copy(whole, whole, sem.at[phase, k]).wait()

        @pl.when(k == 4)
        def _():
            pltpu.make_async_copy(most, most, sem.at[phase, k]).wait()

    def own(k, src, dst):
        @pl.when(k == 4)
        def _():
            dst[4 * 8 + me] = src[4 * 8 + me]

    def put_rows(buf, k, rows_f32, slots):
        for m in range(8):
            buf[k * 8 + m] = rows_f32[m * slots : (m + 1) * slots, :].astype(BF)

    def get_rows(buf, k, slots):
        return buf[pl.ds(k * 8, 8)].astype(F32).reshape(8 * slots, W)

    def loop(body, first=0, last=9):
        def step(t, carry):
            body(chunk_of(t))
            return carry

        lax.fori_loop(first, last, step, 0)

    def enc_make(k):
        @pl.when(valid(k, 1))
        def _():
            rows = dot(pick(T_ENC_CELL, k, EROWS, CELLS), grid_latent[...])
            put_rows(es, k, rows * column(T_ENC_SCALE, k, EROWS), SEP)

    loop(enc_make, 0, 3)
    pl.semaphore_wait(barrier, peers)

    def enc_send(k):
        @pl.when(valid(k, 1))
        def _():
            send(0, k, es, ed, 1)
            own(k, es, ed)

    def enc_both(k):
        enc_make(k)
        enc_send(k)

    loop(enc_send, 0, 3)
    loop(enc_both, 3, 9)

    acc_n[...] = jnp.zeros_like(acc_n)

    def enc_take(k):
        @pl.when(valid(k, -1))
        def _():
            await_bytes(rsem, 0, k, ed)
            rows = get_rows(ed, k, SEP).astype(BF)
            acc_n[...] += dot(place(T_ENC_NODE, k, NODES, EROWS).astype(BF), rows)

    loop(enc_take)

    for copy in loads[12:]:
        copy.wait()
    aggb[...] = acc_n[...].astype(BF)
    state = mesh_latent[...].astype(F32) + dot(aggb[...], w_enc[...])
    nstate[...] = state
    inv_rms = lax.rsqrt(jnp.mean(state * state, axis=-1, keepdims=True) + 1e-05)
    normed[...] = (state * inv_rms * node_gain[...]).astype(BF)
    activation = dot(normed[...], w_up[...])
    act[...] = activation
    hidden[...] = (activation * sigmoid(activation)).astype(BF)
    nhalf[...] = (nstate[...] + dot(hidden[...], w_down[...])).astype(BF)
    prew[...] = dot(nhalf[...], w_msg[...]).astype(BF)

    def dec_send(k):
        @pl.when(valid(k, 1))
        def _():
            put_rows(ds_, k, dot(pick(T_DEC_NODE, k, DROWS, NODES), prew[...]), SD)
            send(1, k, ds_, dd, 1)
            own(k, ds_, dd)

    loop(dec_send)
    acc_c[...] = jnp.zeros_like(acc_c)

    def dec_take(k):
        @pl.when(valid(k, -1))
        def _():
            await_bytes(rsem, 1, k, dd)
            pre = get_rows(dd, k, SD)
            rows = (column(T_DEC_SCALE, k, DROWS) * (pre * sigmoid(pre))).astype(BF)
            acc_c[...] += dot(place(T_DEC_CELL, k, CELLS, DROWS).astype(BF), rows)

    loop(dec_take)

    for b in range(4):
        at = pl.ds(b * 256, 256)
        gathered = acc_c[at, :].astype(BF)
        gath[at, :] = gathered
        blended = (grid_latent[at, :].astype(F32) + dot(gathered, w_dec[...])).astype(BF)
        blend[at, :] = blended
        output = dot_nt(blended, wo[...])
        weight = cols[0:256, T_AREA + b : T_AREA + b + 1]
        residual = (weight * (output - target[:, at].T)).astype(BF)
        resid[at, :] = residual
        back = dot(residual, wo[...])
        grid_grad[at, :] = back
        half = back.astype(BF)
        bhalf[at, :] = half
        bgath[at, :] = dot_nt(half, w_dec[...]).astype(BF)

    def back_send(k):
        @pl.when(valid(k, -1))
        def _():
            pre = get_rows(dd, k, SD)
            rows = dot(pick(T_DEC_CELL, k, DROWS, CELLS), bgath[...])
            put_rows(bs, k, rows * column(T_DEC_SCALE, k, DROWS) * slope(pre), SD)
            send(2, k, bs, bd, -1)
            own(k, bs, bd)

    loop(back_send)

    def to(src, dst, slot, where):
        copy = pltpu.make_async_remote_copy(
            src_ref=src,
            dst_ref=dst,
            send_sem=gs.at[slot],
            recv_sem=gr.at[slot],
            device_id=where,
            device_id_type=MESH_ID,
        )
        copy.start()
        sent.append(copy)
        return copy

    def over_lat(src, dst, slot):
        return [
            to(src.at[lax.rem(la + d, 4)], dst.at[d - 1], slot + d, device(d, 0, me))
            for d in (2, 1, 3)
        ]

    def over_lon(src, dst, slot):
        return [
            to(src.at[lax.rem(lo + d, 4)], dst.at[d - 1], slot + d, device(0, d, me))
            for d in (2, 1, 3)
        ]

    def arrived(copies):
        for copy in copies:
            copy.wait_recv()

    sent = []
    partner = device(0, 0, me + 1 - 2 * core)
    scale = 1.0 / CELLS
    grad = (dot_tn(gath[...], bhalf[...]) * scale).astype(BF)
    ga[0] = grad[:, 0:384]
    ga[1, :, 0:128] = grad[:, 384:512]
    ga[1, :, 128:256] = (dot_tn(blend[...], resid[...]) * scale).astype(BF)
    ga[1, :, 256:384] = jnp.zeros((W, 128), BF)
    arrived([to(ga.at[1 - core], la_c, 0, partner)])
    for j in range(4):
        rows = pl.ds(j * 128, 128)
        ha[j] = (ga[core, rows, :].astype(F32) + la_c[rows, :].astype(F32)).astype(BF)
    wait_a = over_lat(ha, la_y, 0)

    acc_n[...] = jnp.zeros_like(acc_n)

    def back_take(k):
        @pl.when(valid(k, 1))
        def _():
            await_bytes(rsem, 2, k, bd)
            rows = get_rows(bd, k, SD).astype(BF)
            acc_n[...] += dot(place(T_DEC_NODE, k, NODES, DROWS).astype(BF), rows)

    loop(back_take)

    back_pre = acc_n[...].astype(BF)
    back_node = dot_nt(back_pre, w_msg[...])
    back_node_half = back_node.astype(BF)
    back_act = (dot_nt(back_node_half, w_down[...]) * slope(act[...])).astype(BF)
    back_norm = dot_nt(back_act, w_up[...]) * node_gain[...]
    state = nstate[...]
    inv_rms = lax.rsqrt(jnp.mean(state * state, axis=-1, keepdims=True) + 1e-05)
    mean_term = jnp.mean(state * back_norm, axis=-1, keepdims=True)
    back_state = back_node + inv_rms * back_norm - state * (inv_rms * inv_rms * inv_rms * mean_term)
    back_half = back_state.astype(BF)
    prew[...] = dot_nt(back_half, w_enc[...]).astype(BF)

    def enc_back_send(k):
        @pl.when(valid(k, -1))
        def _():
            put_rows(fs, k, dot(pick(T_ENC_NODE, k, EROWS, NODES), prew[...]), SEP)
            send(3, k, fs, fd, -1)
            own(k, fs, fd)

    gb[0, :, 0:512] = (dot_tn(nhalf[...], back_pre) * scale).astype(BF)
    gb[0, :, 512:1024] = (dot_tn(hidden[...], back_node_half) * scale).astype(BF)
    gb[1, :, 0:512] = (dot_tn(normed[...], back_act) * scale).astype(BF)
    gb[1, :, 512:1024] = (dot_tn(aggb[...], back_half) * scale).astype(BF)
    wait_b = [to(gb.at[1 - core], lb_c, 4, partner)]

    loop(enc_back_send, 0, 3)

    arrived(wait_b)
    for j in range(4):
        rows = pl.ds(j * 128, 128)
        both = gb[core, rows, :].astype(F32) + lb_c[rows, :].astype(F32)
        hu[j] = both[:, 0:512].astype(BF)
        for i in range(4):
            hv[i, j] = both[i * 32 : (i + 1) * 32, 512:1024].astype(BF)
    wait_u = over_lat(hu, lu_y, 4)
    wait_v = over_lon(hv, lv_z, 8)
    arrived(wait_a)
    total = ha[la].astype(F32) + la_y[0].astype(F32) + la_y[1].astype(F32) + la_y[2].astype(F32)
    for j in range(4):
        ha2[j] = total[j * 32 : (j + 1) * 32, :].astype(BF)
    wait_a = over_lon(ha2, la_z, 12)

    loop(enc_back_send, 3, 6)

    arrived(wait_u)
    total = hu[la].astype(F32) + lu_y[0].astype(F32) + lu_y[1].astype(F32) + lu_y[2].astype(F32)
    for j in range(4):
        hu2[j] = total[j * 32 : (j + 1) * 32, :].astype(BF)
    wait_u = over_lon(hu2, lu_z, 16)
    arrived(wait_v)
    for j in range(4):
        total = hv[lo, j].astype(F32) + lv_z[0, j].astype(F32)
        hv2[j] = (total + lv_z[1, j].astype(F32) + lv_z[2, j].astype(F32)).astype(BF)
    wait_v = over_lat(hv2, lv_y, 20)

    loop(enc_back_send, 6, 9)

    def finished(own_part, landed):
        total = own_part.astype(F32) + landed[0].astype(F32)
        return total + landed[1].astype(F32) + landed[2].astype(F32)

    arrived(wait_u)
    arrived(wait_v)
    arrived(wait_a)
    for at, total in (
        (0, finished(hu2[lo], lu_z)),
        (512, finished(hv2[la], lv_y)),
        (1024, finished(ha2[lo], la_z)),
    ):
        for j in range(8):
            hm[j, :, at : at + total.shape[1]] = total[j * 4 : (j + 1) * 4, :]
    wait_m = []
    for d in (4, 3, 5, 2, 6, 1, 7):
        part = lax.rem(me + d, 8)
        wait_m.append(to(hm.at[part], lm.at[d - 1], 24 + d, device(0, 0, part)))

    def enc_back_take(k):
        @pl.when(valid(k, 1))
        def _():
            await_bytes(rsem, 3, k, fd)
            rows = get_rows(fd, k, SEP).astype(BF)
            weight = table[pl.ds(T_ENC_SCALE + k, 1), :][:, 0:EROWS]
            spread = (place(T_ENC_CELL, k, CELLS, EROWS) * weight).astype(BF)
            grid_grad[...] += dot(spread, rows)

    loop(enc_back_take)

    arrived(wait_m)
    same = hm[me]
    other = lm[0]
    same = same + lm[1] + lm[3] + lm[5]
    other = other + lm[2] + lm[4] + lm[6]
    low = jnp.where(core == 0, same, other)
    high = jnp.where(core == 0, other, same)
    g_msg[...] = low[:, 0:512]
    g_down[...] = low[:, 512:1024]
    g_dec[:, 0:384] = low[:, 1024:1408]
    g_up[...] = high[:, 0:512]
    g_enc[...] = high[:, 512:1024]
    g_dec[:, 384:512] = high[:, 1024:1152]
    g_out[...] = high[:, 1152 : 1152 + 84]

    for c in sent:
        c.wait_send()

    def drain(k):
        @pl.when(valid(k, 1))
        def _():
            await_bytes(ssem, 0, k, es)
            await_bytes(ssem, 1, k, ds_)

        @pl.when(valid(k, -1))
        def _():
            await_bytes(ssem, 2, k, bs)
            await_bytes(ssem, 3, k, fs)

    loop(drain)


def scratch():
    v = pltpu.VMEM
    return [
        v((9, 8, SE), jnp.int32),
        v((9, 8, SE), jnp.int32),
        v((9, 8, SD), jnp.int32),
        v((9, 8, SD), jnp.int32),
        v((9, 8, SE), F32),
        v((9, 8, SD), F32),
        v((9, 1, 8), jnp.int32),
        v((8, 128), F32),
        v((84, CELLS), BF),
        v((84, W), BF),
        v((1, W), F32),
        v((CELLS, W), BF),
        v((NODES, W), BF),
        v((W, W), BF),
        v((W, W), BF),
        v((W, W), BF),
        v((W, W), BF),
        v((W, W), BF),
        v((128, CELLS), F32),
        v((8, 256), F32),
        v((128, 256), F32),
        v((256, 128), F32),
        v((72, SEP, W), BF),
        v((72, SEP, W), BF),
        v((72, SD, W), BF),
        v((72, SD, W), BF),
        v((72, SD, W), BF),
        v((72, SD, W), BF),
        v((72, SEP, W), BF),
        v((72, SEP, W), BF),
        v((NODES, W), F32),
        v((CELLS, W), F32),
        v((CELLS, W), BF),
        v((CELLS, W), BF),
        v((CELLS, W), BF),
        v((CELLS, W), BF),
        v((CELLS, 128), BF),
        v((128, W), BF),
        v((NODES, W), F32),
        v((NODES, W), F32),
        v((NODES, W), BF),
        v((NODES, W), BF),
        v((NODES, W), BF),
        v((NODES, W), BF),
        v((NODES, W), BF),
        v((2, W, 384), BF),
        v((W, 384), BF),
        v((4, 128, 384), BF),
        v((3, 128, 384), BF),
        v((4, 32, 384), BF),
        v((3, 32, 384), BF),
        v((2, W, 1024), BF),
        v((W, 1024), BF),
        v((4, 128, 512), BF),
        v((3, 128, 512), BF),
        v((4, 32, 512), BF),
        v((3, 32, 512), BF),
        v((4, 4, 32, 512), BF),
        v((3, 4, 32, 512), BF),
        v((4, 32, 512), BF),
        v((3, 32, 512), BF),
        v((8, 4, 1408), F32),
        v((7, 4, 1408), F32),
        pltpu.SemaphoreType.DMA((4, 9)),
        pltpu.SemaphoreType.DMA((4, 9)),
        pltpu.SemaphoreType.DMA((32,)),
        pltpu.SemaphoreType.DMA((32,)),
        pltpu.SemaphoreType.DMA((18,)),
    ]


def on_device(
    grid_latent,
    target,
    area,
    mesh_latent,
    node_gain,
    w_enc,
    w_up,
    w_down,
    w_msg,
    w_dec,
    w_out,
    enc_cell,
    enc_live,
    enc_weight,
    enc_node,
    dec_node,
    dec_cell,
    dec_weight,
):
    vm = pl.BlockSpec(memory_space=pltpu.VMEM)
    small = jax.ShapeDtypeStruct((4, W), F32)
    any_space = pl.BlockSpec(memory_space=pl.ANY)
    shapes = (jax.ShapeDtypeStruct((CELLS, W), F32),) + (small,) * 5
    shapes += (jax.ShapeDtypeStruct((4, 84), F32),)
    outs = pl.pallas_call(
        kernel,
        out_shape=shapes,
        in_specs=[any_space] * 18,
        out_specs=(vm,) * 7,
        scratch_shapes=scratch(),
        compiler_params=pltpu.CompilerParams(
            collective_id=0, has_side_effects=True, vmem_limit_bytes=VMEM_LIMIT
        ),
        name="step",
    )(
        enc_cell.reshape(9, 8, SE),
        enc_node.reshape(9, 8, SE),
        dec_node.reshape(9, 8, SD),
        dec_cell.reshape(9, 8, SD),
        enc_weight.reshape(9, 8, SE),
        dec_weight.reshape(9, 8, SD),
        enc_live.reshape(9, 1, 8),
        area.reshape(8, 128),
        target.T,
        w_out.T,
        node_gain.reshape(1, W),
        grid_latent,
        mesh_latent,
        w_enc,
        w_up,
        w_down,
        w_msg,
        w_dec,
    )
    return pl.pallas_call(
        finish,
        out_shape=shapes,
        in_specs=[any_space] * 7,
        out_specs=(any_space,) * 7,
        scratch_shapes=[
            pltpu.VMEM((CELLS, W), F32),
            pltpu.VMEM((5, 4, W), F32),
            pltpu.VMEM((4, 84), F32),
            pltpu.SemaphoreType.DMA((10,)),
            pltpu.SemaphoreType.DMA((10,)),
        ],
        compiler_params=pltpu.CompilerParams(vmem_limit_bytes=VMEM_LIMIT),
        name="finish",
    )(*outs)


def finish(*refs):
    grid, small, head, arrive, leave = refs[14:]
    parts = [
        (refs[0].at[rows], grid.at[rows], refs[7].at[rows])
        for rows in (pl.ds(b * 256, 256) for b in range(4))
    ]
    parts += [(refs[i], small.at[i - 1], refs[7 + i]) for i in range(1, 6)]
    parts.append((refs[6], head, refs[13]))
    inward = [pltpu.make_async_copy(a, b, arrive.at[i]) for i, (a, b, c) in enumerate(parts)]
    outward = [pltpu.make_async_copy(b, c, leave.at[i]) for i, (a, b, c) in enumerate(parts)]
    for copy in inward:
        copy.start()
    for first, second in zip(inward, outward):
        first.wait()
        second.start()
    for copy in outward:
        copy.wait()


def solution(mesh):
    rows = P(AXES, None)
    slots = P(AXES, None, None, None, None)
    in_specs = (
        rows,
        rows,
        P(AXES),
        rows,
        P(),
        P(),
        P(),
        P(),
        P(),
        P(),
        P(),
        slots,
        P(AXES, None, None, None),
        slots,
        slots,
        slots,
        slots,
        slots,
    )
    return jax.shard_map(
        on_device, mesh=mesh, in_specs=in_specs, out_specs=(rows,) * 7, check_vma=False
    )
```

time: 547 us -> 136 us (0.25); the launches traced: 537 us -> 134 us
  waiting for transfers between devices: 158 us -> 0 us
  blocking collectives: 135 us -> 0 us
  Pallas kernels: 0 us -> 133 us
  local copies, waits for them, and re-layouts: 95.1 us -> 0 us
  other arithmetic: 87 us -> 0 us
  starting transfers between devices: 31.8 us -> 0 us
  matrix products: 28.1 us -> 0 us
    ppermute x16 -> x0, waiting for transfers between devices: 141 us -> none  [the longest x8 140 us: extended_2(): lax.ppermute(tail, axis, [(i, (i + 1) % count) for i in range(count)])]
    all_to_all x5 -> x0, blocking collectives: 135 us -> none  [the longest x2 68.9 us: route_dec(): lax.all_to_all(bucket, MESH, split_axis=2, concat_axis=2, tiled=True)]
    pallas_call x0 -> x2, Pallas kernels: none -> 133 us  [the longest x1 131 us: on_device(): pl.pallas_call(kernel, out_shape=shapes, in_specs=[any_space] * 18, out_s...]
    scatter-add x4 -> x0, other arithmetic: 57.1 us -> none  [the longest x1 19.1 us: on_device(): jax.ops.segment_sum(weighted, cell_ids, num_segments=cell_rows)]
    gather x6 -> x0, local copies, waits for them, and re-layouts: 29.3 us -> none  [the longest x2 9.34 us: on_device(): leaving = node_half[dec_node[0]]]
    dot_general x18 -> x0, matrix products: 28.1 us -> none  [the longest x12 17 us: matmul(): return jnp.dot(left, right, preferred_element_type=jnp.float32)]
    ppermute x16 -> x0, starting transfers between devices: 23.9 us -> none  [the longest x8 16.6 us: extended_2(): lax.ppermute(head, axis, [((i + 1) % count, i) for i in range(count)])]
    all_to_all x1 -> x0, waiting for transfers between devices: 17.6 us -> none  [sum_in_two_steps(): lax.all_to_all(nearer.astype(jnp.bfloat16), far, split_axis=0, concat_axi...]
  transfers between devices with their start and end apart: 17 -> 0, of which waited for: 10 -> 0; matrix products, arithmetic and copies ran while one was open for 2% -> 0% of each run, Pallas kernels for 0% -> 0%
where the time goes in v1:
time: 136 us; the launch traced here: 134 us
  Pallas kernels  133 us (98%)
    pallas_call x1, Pallas kernels, on_device(): pl.pallas_call(kernel, out_shape=shapes, in_specs=[any_space] * 18, out_s...  131 us

profile of v1, /device:TPU:1, one launch (start us, length us, event | category | flops | bytes accessed | tf_op | source)
XLA Modules:
  0.0 133.8 jit_solution(6812036341118937858)
XLA Ops:
  0.6 130.6 %step.1 = (f32[1024,512]{1,0:T(8,128)}, f32[4,512]{1,0:T(4,128)}, f32[4,512]{1,0:T(4,128)}, f32[4,512]{1,0:T(4,128)}, f32[4,512]{1,0:T(4,128)}, /*index=5*/f32[4,512]{1,0:T(4,128)}, f32[4,84]{1,0:T(4,128)}) custom-call(s32[9,8,21]{2,1,0:T(8,128)} %bitcast.13, s32[9,8,21]{2,1,0:T(8,128)} %bitcast.14, s32[9,8,32]{2,1,0:T(8,128)} %bitcast.15, ...), custom_call_target="tpu_custom_call" | custom-call | tf_op jit(solution)/shard_map/step/pallas_call | solution.py:672
  131.2 2.5 %finish.1 = (f32[1024,512]{1,0:T(8,128)}, f32[4,512]{1,0:T(4,128)}, f32[4,512]{1,0:T(4,128)}, f32[4,512]{1,0:T(4,128)}, f32[4,512]{1,0:T(4,128)}, /*index=5*/f32[4,512]{1,0:T(4,128)}, f32[4,84]{1,0:T(4,128)}) custom-call(f32[1024,512]{1,0:T(8,128)} %get-tuple-element.14.refs_0_, f32[4,512]{1,0:T(4,128)} %get-tuple-element.15.refs_1_, ...), custom_call_target="tpu_custom_call" | custom-call | tf_op jit(solution)/shard_map/finish/pallas_call | solution.py:702

commit v2 on v1

--- a/solution.py
+++ b/solution.py
@@ -98,6 +98,11 @@
     pad,
     table,
     cols,
+    by_part,
+    far_part,
+    far_rows,
+    far_out,
+    backw,
     es,
     ed,
     ds_,
@@ -147,6 +152,8 @@
 ):
     la, lo, me = lax.axis_index("lat"), lax.axis_index("lon"), lax.axis_index("mesh")
     core = lax.rem(me, 2)
+    far_same = lax.rem(me + 4, 8)
+    far_other = far_same + 1 - 2 * core
 
     def device(dla, dlo, part):
         return {"lat": lax.rem(la + dla, 4), "lon": lax.rem(lo + dlo, 4), "mesh": part}
@@ -212,6 +219,8 @@
             table[pl.ds(block + k, 1), :] = row
 
         put(T_DEC_NODE, dec_node[k].astype(F32), SD, SD)
+        for m in range(8):
+            by_part[m, pl.ds(k, 1), :] = pad[m : m + 1, 0:128]
         put(T_DEC_CELL, dec_cell[k].astype(F32), SD, SD)
         put(T_DEC_SCALE, dec_weight[k], SD, SD)
         pad[...] = jnp.zeros_like(pad)
@@ -255,10 +264,32 @@
         at = la + sign * (k // 3 - 1)
         return (at >= 0) & (at < 4)
 
+    def to(src, dst, slot, where):
+        copy = pltpu.make_async_remote_copy(
+            src_ref=src,
+            dst_ref=dst,
+            send_sem=gs.at[slot],
+            recv_sem=gr.at[slot],
+            device_id=where,
+            device_id_type=MESH_ID,
+        )
+        copy.start()
+        sent.append(copy)
+        return copy
+
+    def arrived(copies):
+        for copy in copies:
+            copy.wait_recv()
+
+    sent = []
+    partner = device(0, 0, me + 1 - 2 * core)
+
     def send(phase, k, src, dst, sign):
         dla = k // 3 - 1
         dlo = lax.rem(k, 3) - 1
         for d in (4, 3, 5, 2, 6, 1, 7, 0):
+            if phase == 1 and d in (3, 4, 5):
+                continue
             part = lax.rem(me + d, 8)
             copy = pltpu.make_async_remote_copy(
                 src_ref=src.at[k * 8 + part],
@@ -272,10 +303,20 @@
                 pl.when(k != 4)(copy.start)
             else:
                 copy.start()
+        if phase == 1:
+            part = lax.rem(me + 3 + 2 * core, 8)
+            pltpu.make_async_remote_copy(
+                src_ref=src.at[k * 8 + part],
+                dst_ref=dst.at[k * 8 + me],
+                send_sem=ssem.at[phase, k],
+                recv_sem=rsem.at[phase, k],
+                device_id=device(sign * dla + 4, sign * dlo + 4, part),
+                device_id_type=MESH_ID,
+            ).start()
 
     def await_bytes(sem, phase, k, buf):
         whole = buf.at[pl.ds(k * 8, 8)]
-        most = buf.at[pl.ds(k * 8, 7)]
+        most = buf.at[pl.ds(k * 8, 5 if phase == 1 else 7)]
 
         @pl.when(k != 4)
         def _():
@@ -324,6 +365,10 @@
         enc_send(k)
 
     loop(enc_send, 0, 3)
+    far_tables = [
+        to(by_part.at[far_same], far_part.at[0], 27, device(0, 0, far_same)),
+        to(by_part.at[far_other], far_part.at[1], 28, device(0, 0, far_other)),
+    ]
     loop(enc_both, 3, 9)
 
     acc_n[...] = jnp.zeros_like(acc_n)
@@ -357,7 +402,39 @@
             send(1, k, ds_, dd, 1)
             own(k, ds_, dd)
 
+    far_block = to(prew, far_rows.at[0], 29, device(0, 0, far_same))
     loop(dec_send)
+
+    def relay(i, source):
+        turned = far_part[i].T
+        index = jnp.concatenate([turned[0:SD, k : k + 1] for k in range(9)], axis=0)
+        width = lax.broadcasted_iota(jnp.int32, (9 * SD, NODES), 1)
+        chosen = (index.astype(jnp.int32) == width).astype(F32).astype(BF)
+        rows = dot(chosen, far_rows[i]).astype(BF)
+        for k in range(9):
+            far_out[i * 9 + k] = rows[k * SD : (k + 1) * SD, :]
+
+        def relay_send(k):
+            @pl.when(valid(k, 1) & (k != 4))
+            def _():
+                pltpu.make_async_remote_copy(
+                    src_ref=far_out.at[i * 9 + k],
+                    dst_ref=dd.at[k * 8 + source],
+                    send_sem=ssem.at[1, k],
+                    recv_sem=rsem.at[1, k],
+                    device_id=device(k // 3 + 3, lax.rem(k, 3) + 3, me),
+                    device_id_type=MESH_ID,
+                ).start()
+
+        loop(relay_send)
+        dd[4 * 8 + source] = far_out[i * 9 + 4]
+
+    arrived(far_tables)
+    arrived([far_block])
+    far_block = to(far_rows.at[0], far_rows.at[1], 30, partner)
+    relay(0, far_same)
+    arrived([far_block])
+    relay(1, far_other)
     acc_c[...] = jnp.zeros_like(acc_c)
 
     def dec_take(k):
@@ -397,19 +474,6 @@
 
     loop(back_send)
 
-    def to(src, dst, slot, where):
-        copy = pltpu.make_async_remote_copy(
-            src_ref=src,
-            dst_ref=dst,
-            send_sem=gs.at[slot],
-            recv_sem=gr.at[slot],
-            device_id=where,
-            device_id_type=MESH_ID,
-        )
-        copy.start()
-        sent.append(copy)
-        return copy
-
     def over_lat(src, dst, slot):
         return [
             to(src.at[lax.rem(la + d, 4)], dst.at[d - 1], slot + d, device(d, 0, me))
@@ -422,12 +486,6 @@
             for d in (2, 1, 3)
         ]
 
-    def arrived(copies):
-        for copy in copies:
-            copy.wait_recv()
-
-    sent = []
-    partner = device(0, 0, me + 1 - 2 * core)
     scale = 1.0 / CELLS
     grad = (dot_tn(gath[...], bhalf[...]) * scale).astype(BF)
     ga[0] = grad[:, 0:384]
@@ -461,12 +519,12 @@
     mean_term = jnp.mean(state * back_norm, axis=-1, keepdims=True)
     back_state = back_node + inv_rms * back_norm - state * (inv_rms * inv_rms * inv_rms * mean_term)
     back_half = back_state.astype(BF)
-    prew[...] = dot_nt(back_half, w_enc[...]).astype(BF)
+    backw[...] = dot_nt(back_half, w_enc[...]).astype(BF)
 
     def enc_back_send(k):
         @pl.when(valid(k, -1))
         def _():
-            put_rows(fs, k, dot(pick(T_ENC_NODE, k, EROWS, NODES), prew[...]), SEP)
+            put_rows(fs, k, dot(pick(T_ENC_NODE, k, EROWS, NODES), backw[...]), SEP)
             send(3, k, fs, fd, -1)
             own(k, fs, fd)
 
@@ -525,7 +583,7 @@
     wait_m = []
     for d in (4, 3, 5, 2, 6, 1, 7):
         part = lax.rem(me + d, 8)
-        wait_m.append(to(hm.at[part], lm.at[d - 1], 24 + d, device(0, 0, part)))
+        wait_m.append(to(hm.at[part], lm.at[d - 1], 32 + d, device(0, 0, part)))
 
     def enc_back_take(k):
         @pl.when(valid(k, 1))
@@ -595,6 +653,11 @@
         v((8, 256), F32),
         v((128, 256), F32),
         v((256, 128), F32),
+        v((8, 16, 128), F32),
+        v((2, 16, 128), F32),
+        v((2, NODES, W), BF),
+        v((18, SD, W), BF),
+        v((NODES, W), BF),
         v((72, SEP, W), BF),
         v((72, SEP, W), BF),
         v((72, SD, W), BF),
@@ -638,8 +701,8 @@
         v((7, 4, 1408), F32),
         pltpu.SemaphoreType.DMA((4, 9)),
         pltpu.SemaphoreType.DMA((4, 9)),
-        pltpu.SemaphoreType.DMA((32,)),
-        pltpu.SemaphoreType.DMA((32,)),
+        pltpu.SemaphoreType.DMA((40,)),
+        pltpu.SemaphoreType.DMA((40,)),
         pltpu.SemaphoreType.DMA((18,)),
     ]
 

time: 136 us -> 134 us (0.985)
    pallas_call x1, Pallas kernels: 131 us -> 129 us  [on_device(): pl.pallas_call(kernel, out_shape=shapes, in_specs=[any_space] * 18, out_s...]
where the time goes in v2:
time: 134 us; the launch traced here: 132 us
  Pallas kernels  132 us (99%)
    pallas_call x1, Pallas kernels, on_device(): pl.pallas_call(kernel, out_shape=shapes, in_specs=[any_space] * 18, out_s...  129 us

profile of v2, /device:TPU:1, one launch (start us, length us, event | category | flops | bytes accessed | tf_op | source)
XLA Modules:
  0.0 132.2 jit_solution(10418587765493864220)
XLA Ops:
  0.6 129.0 %step.1 = (f32[1024,512]{1,0:T(8,128)}, f32[4,512]{1,0:T(4,128)}, f32[4,512]{1,0:T(4,128)}, f32[4,512]{1,0:T(4,128)}, f32[4,512]{1,0:T(4,128)}, /*index=5*/f32[4,512]{1,0:T(4,128)}, f32[4,84]{1,0:T(4,128)}) custom-call(s32[9,8,21]{2,1,0:T(8,128)} %bitcast.13, s32[9,8,21]{2,1,0:T(8,128)} %bitcast.14, s32[9,8,32]{2,1,0:T(8,128)} %bitcast.15, ...), custom_call_target="tpu_custom_call" | custom-call | tf_op jit(solution)/shard_map/step/pallas_call | solution.py:735
  129.7 2.5 %finish.1 = (f32[1024,512]{1,0:T(8,128)}, f32[4,512]{1,0:T(4,128)}, f32[4,512]{1,0:T(4,128)}, f32[4,512]{1,0:T(4,128)}, f32[4,512]{1,0:T(4,128)}, /*index=5*/f32[4,512]{1,0:T(4,128)}, f32[4,84]{1,0:T(4,128)}) custom-call(f32[1024,512]{1,0:T(8,128)} %get-tuple-element.14.refs_0_, f32[4,512]{1,0:T(4,128)} %get-tuple-element.15.refs_1_, ...), custom_call_target="tpu_custom_call" | custom-call | tf_op jit(solution)/shard_map/finish/pallas_call | solution.py:765

commit v3 on v2

--- a/solution.py
+++ b/solution.py
@@ -69,7 +69,7 @@
     w_down_in,
     w_msg_in,
     w_dec_in,
-    grid_grad,
+    grid_out,
     g_enc,
     g_up,
     g_down,
@@ -98,6 +98,9 @@
     pad,
     table,
     cols,
+    grid_grad,
+    grid_half,
+    os_,
     by_part,
     far_part,
     far_rows,
@@ -528,13 +531,14 @@
             send(3, k, fs, fd, -1)
             own(k, fs, fd)
 
+    loop(enc_back_send, 0, 5)
+
     gb[0, :, 0:512] = (dot_tn(nhalf[...], back_pre) * scale).astype(BF)
     gb[0, :, 512:1024] = (dot_tn(hidden[...], back_node_half) * scale).astype(BF)
     gb[1, :, 0:512] = (dot_tn(normed[...], back_act) * scale).astype(BF)
     gb[1, :, 512:1024] = (dot_tn(aggb[...], back_half) * scale).astype(BF)
     wait_b = [to(gb.at[1 - core], lb_c, 4, partner)]
-
-    loop(enc_back_send, 0, 3)
+    loop(enc_back_send, 5, 9)
 
     arrived(wait_b)
     for j in range(4):
@@ -551,8 +555,6 @@
         ha2[j] = total[j * 32 : (j + 1) * 32, :].astype(BF)
     wait_a = over_lon(ha2, la_z, 12)
 
-    loop(enc_back_send, 3, 6)
-
     arrived(wait_u)
     total = hu[la].astype(F32) + lu_y[0].astype(F32) + lu_y[1].astype(F32) + lu_y[2].astype(F32)
     for j in range(4):
@@ -564,8 +566,6 @@
         hv2[j] = (total + lv_z[1, j].astype(F32) + lv_z[2, j].astype(F32)).astype(BF)
     wait_v = over_lat(hv2, lv_y, 20)
 
-    loop(enc_back_send, 6, 9)
-
     def finished(own_part, landed):
         total = own_part.astype(F32) + landed[0].astype(F32)
         return total + landed[1].astype(F32) + landed[2].astype(F32)
@@ -579,7 +579,7 @@
         (1024, finished(ha2[lo], la_z)),
     ):
         for j in range(8):
-            hm[j, :, at : at + total.shape[1]] = total[j * 4 : (j + 1) * 4, :]
+            hm[j, :, at : at + total.shape[1]] = total[j * 4 : (j + 1) * 4, :].astype(BF)
     wait_m = []
     for d in (4, 3, 5, 2, 6, 1, 7):
         part = lax.rem(me + d, 8)
@@ -594,13 +594,27 @@
             spread = (place(T_ENC_CELL, k, CELLS, EROWS) * weight).astype(BF)
             grid_grad[...] += dot(spread, rows)
 
-    loop(enc_back_take)
+    loop(enc_back_take, 0, 8)
+
+    await_bytes(rsem, 3, 4, fd)
+    rows = get_rows(fd, 4, SEP).astype(BF)
+    weight = table[T_ENC_SCALE + 4 : T_ENC_SCALE + 5, 0:EROWS]
+    index = table[T_ENC_CELL + 4 : T_ENC_CELL + 5, 0:EROWS].astype(jnp.int32)
+    leave = []
+    for b in range(4):
+        at = pl.ds(b * 256, 256)
+        here = index == lax.broadcasted_iota(jnp.int32, (256, EROWS), 0) + b * 256
+        spread = (here.astype(F32) * weight).astype(BF)
+        grid_half[at, :] = (grid_grad[at, :] + dot(spread, rows)).astype(BF)
+        leave.append(pltpu.make_async_copy(grid_half.at[at], grid_out.at[at], os_.at[b]))
+        leave[b].start()
 
     arrived(wait_m)
-    same = hm[me]
-    other = lm[0]
-    same = same + lm[1] + lm[3] + lm[5]
-    other = other + lm[2] + lm[4] + lm[6]
+    landed = [lm[d].astype(F32) for d in range(7)]
+    same = hm[me].astype(F32)
+    other = landed[0]
+    same = same + landed[1] + landed[3] + landed[5]
+    other = other + landed[2] + landed[4] + landed[6]
     low = jnp.where(core == 0, same, other)
     high = jnp.where(core == 0, other, same)
     g_msg[...] = low[:, 0:512]
@@ -613,6 +627,8 @@
 
     for c in sent:
         c.wait_send()
+    for c in leave:
+        c.wait()
 
     def drain(k):
         @pl.when(valid(k, 1))
@@ -653,6 +669,9 @@
         v((8, 256), F32),
         v((128, 256), F32),
         v((256, 128), F32),
+        v((CELLS, W), F32),
+        v((CELLS, W), BF),
+        pltpu.SemaphoreType.DMA((4,)),
         v((8, 16, 128), F32),
         v((2, 16, 128), F32),
         v((2, NODES, W), BF),
@@ -697,8 +716,8 @@
         v((3, 4, 32, 512), BF),
         v((4, 32, 512), BF),
         v((3, 32, 512), BF),
-        v((8, 4, 1408), F32),
-        v((7, 4, 1408), F32),
+        v((8, 4, 1408), BF),
+        v((7, 4, 1408), BF),
         pltpu.SemaphoreType.DMA((4, 9)),
         pltpu.SemaphoreType.DMA((4, 9)),
         pltpu.SemaphoreType.DMA((40,)),
@@ -730,13 +749,12 @@
     vm = pl.BlockSpec(memory_space=pltpu.VMEM)
     small = jax.ShapeDtypeStruct((4, W), F32)
     any_space = pl.BlockSpec(memory_space=pl.ANY)
-    shapes = (jax.ShapeDtypeStruct((CELLS, W), F32),) + (small,) * 5
-    shapes += (jax.ShapeDtypeStruct((4, 84), F32),)
+    rest = (small,) * 5 + (jax.ShapeDtypeStruct((4, 84), F32),)
     outs = pl.pallas_call(
         kernel,
-        out_shape=shapes,
+        out_shape=(jax.ShapeDtypeStruct((CELLS, W), BF),) + rest,
         in_specs=[any_space] * 18,
-        out_specs=(vm,) * 7,
+        out_specs=(any_space,) + (vm,) * 6,
         scratch_shapes=scratch(),
         compiler_params=pltpu.CompilerParams(
             collective_id=0, has_side_effects=True, vmem_limit_bytes=VMEM_LIMIT
@@ -764,10 +782,11 @@
     )
     return pl.pallas_call(
         finish,
-        out_shape=shapes,
+        out_shape=(jax.ShapeDtypeStruct((CELLS, W), F32),) + rest,
         in_specs=[any_space] * 7,
         out_specs=(any_space,) * 7,
         scratch_shapes=[
+            pltpu.VMEM((CELLS, W), BF),
             pltpu.VMEM((CELLS, W), F32),
             pltpu.VMEM((5, 4, W), F32),
             pltpu.VMEM((4, 84), F32),
@@ -780,20 +799,21 @@
 
 
 def finish(*refs):
-    grid, small, head, arrive, leave = refs[14:]
-    parts = [
-        (refs[0].at[rows], grid.at[rows], refs[7].at[rows])
-        for rows in (pl.ds(b * 256, 256) for b in range(4))
-    ]
-    parts += [(refs[i], small.at[i - 1], refs[7 + i]) for i in range(1, 6)]
-    parts.append((refs[6], head, refs[13]))
-    inward = [pltpu.make_async_copy(a, b, arrive.at[i]) for i, (a, b, c) in enumerate(parts)]
-    outward = [pltpu.make_async_copy(b, c, leave.at[i]) for i, (a, b, c) in enumerate(parts)]
+    half, full, small, head, arrive, leave = refs[14:]
+    blocks = [pl.ds(b * 256, 256) for b in range(4)]
+    inward = [(refs[0].at[rows], half.at[rows]) for rows in blocks]
+    inward += [(refs[i], small.at[i - 1]) for i in range(1, 6)] + [(refs[6], head)]
+    outward = [(full.at[rows], refs[7].at[rows]) for rows in blocks]
+    outward += [(small.at[i - 1], refs[7 + i]) for i in range(1, 6)] + [(head, refs[13])]
+    inward = [pltpu.make_async_copy(a, b, arrive.at[i]) for i, (a, b) in enumerate(inward)]
+    outward = [pltpu.make_async_copy(a, b, leave.at[i]) for i, (a, b) in enumerate(outward)]
     for copy in inward:
         copy.start()
-    for first, second in zip(inward, outward):
-        first.wait()
-        second.start()
+    for i in range(10):
+        inward[i].wait()
+        if i < 4:
+            full[blocks[i], :] = half[blocks[i], :].astype(F32)
+        outward[i].start()
     for copy in outward:
         copy.wait()
 

time: 134 us -> 132 us (0.985); the launches traced: 132 us -> 132 us
  no operation moved by 1% of the time
where the time goes in v3:
time: 132 us
  Pallas kernels  131 us (99%)
    pallas_call x1, Pallas kernels, on_device(): pl.pallas_call(kernel, out_shape=(jax.ShapeDtypeStruct((CELLS, W), BF),)...  129 us

profile of v3, /device:TPU:1, one launch (start us, length us, event | category | flops | bytes accessed | tf_op | source)
XLA Modules:
  0.0 131.6 jit_solution(14559204725424857465)
XLA Ops:
  0.6 128.5 %step.1 = (bf16[1024,512]{1,0:T(8,128)(2,1)}, f32[4,512]{1,0:T(4,128)}, f32[4,512]{1,0:T(4,128)}, f32[4,512]{1,0:T(4,128)}, f32[4,512]{1,0:T(4,128)}, /*index=5*/f32[4,512]{1,0:T(4,128)}, f32[4,84]{1,0:T(4,128)}) custom-call(s32[9,8,21]{2,1,0:T(8,128)} %bitcast.13, s32[9,8,21]{2,1,0:T(8,128)} %bitcast.14, s32[9,8,32]{2,1,0:T(8,128)} %bitcast.15, ...), custom_call_target="tpu_custom_call" | custom-call | tf_op jit(solution)/shard_map/step/pallas_call | solution.py:753
  129.2 2.5 %finish.1 = (f32[1024,512]{1,0:T(8,128)}, f32[4,512]{1,0:T(4,128)}, f32[4,512]{1,0:T(4,128)}, f32[4,512]{1,0:T(4,128)}, f32[4,512]{1,0:T(4,128)}, /*index=5*/f32[4,512]{1,0:T(4,128)}, f32[4,84]{1,0:T(4,128)}) custom-call(bf16[1024,512]{1,0:T(8,128)(2,1)} %get-tuple-element.14.refs_0_, f32[4,512]{1,0:T(4,128)} %get-tuple-element.15.refs_1_, ...), custom_call_target="tpu_custom_call" | custom-call | tf_op jit(solution)/shard_map/finish/pallas_call | solution.py:783

commit v4 on v3

--- a/solution.py
+++ b/solution.py
@@ -106,6 +106,13 @@
     far_rows,
     far_out,
     backw,
+    kept,
+    far_in,
+    part_other,
+    part_in,
+    part_out,
+    far_back,
+    fsem,
     es,
     ed,
     ds_,
@@ -291,7 +298,7 @@
         dla = k // 3 - 1
         dlo = lax.rem(k, 3) - 1
         for d in (4, 3, 5, 2, 6, 1, 7, 0):
-            if phase == 1 and d in (3, 4, 5):
+            if phase in (1, 2) and d in (3, 4, 5):
                 continue
             part = lax.rem(me + d, 8)
             copy = pltpu.make_async_remote_copy(
@@ -306,7 +313,7 @@
                 pl.when(k != 4)(copy.start)
             else:
                 copy.start()
-        if phase == 1:
+        if phase in (1, 2):
             part = lax.rem(me + 3 + 2 * core, 8)
             pltpu.make_async_remote_copy(
                 src_ref=src.at[k * 8 + part],
@@ -317,9 +324,9 @@
                 device_id_type=MESH_ID,
             ).start()
 
-    def await_bytes(sem, phase, k, buf):
-        whole = buf.at[pl.ds(k * 8, 8)]
-        most = buf.at[pl.ds(k * 8, 5 if phase == 1 else 7)]
+    def await_bytes(sem, phase, k, buf, usual=8):
+        whole = buf.at[pl.ds(k * 8, usual)]
+        most = buf.at[pl.ds(k * 8, 5 if phase in (1, 2) else 7)]
 
         @pl.when(k != 4)
         def _():
@@ -413,6 +420,7 @@
         index = jnp.concatenate([turned[0:SD, k : k + 1] for k in range(9)], axis=0)
         width = lax.broadcasted_iota(jnp.int32, (9 * SD, NODES), 1)
         chosen = (index.astype(jnp.int32) == width).astype(F32).astype(BF)
+        kept[i] = chosen
         rows = dot(chosen, far_rows[i]).astype(BF)
         for k in range(9):
             far_out[i * 9 + k] = rows[k * SD : (k + 1) * SD, :]
@@ -472,6 +480,22 @@
             pre = get_rows(dd, k, SD)
             rows = dot(pick(T_DEC_CELL, k, DROWS, CELLS), bgath[...])
             put_rows(bs, k, rows * column(T_DEC_SCALE, k, DROWS) * slope(pre), SD)
+            for i, source in enumerate((far_same, far_other)):
+                copy = pltpu.make_async_remote_copy(
+                    src_ref=bs.at[k * 8 + source],
+                    dst_ref=far_in.at[i * 9 + k],
+                    send_sem=ssem.at[2, k],
+                    recv_sem=fsem.at[i, k],
+                    device_id=device(5 - k // 3, 5 - lax.rem(k, 3), me),
+                    device_id_type=MESH_ID,
+                )
+                pl.when(k != 4)(copy.start)
+
+            @pl.when(k == 4)
+            def _():
+                far_in[4] = bs[4 * 8 + far_same]
+                far_in[9 + 4] = bs[4 * 8 + far_other]
+
             send(2, k, bs, bd, -1)
             own(k, bs, bd)
 
@@ -501,18 +525,43 @@
         ha[j] = (ga[core, rows, :].astype(F32) + la_c[rows, :].astype(F32)).astype(BF)
     wait_a = over_lat(ha, la_y, 0)
 
+    def far_sum(i):
+        def far_take(k):
+            landing = far_in.at[i * 9 + k]
+
+            @pl.when(valid(k, 1) & (k != 4))
+            def _():
+                pltpu.make_async_copy(landing, landing, fsem.at[i, k]).wait()
+
+            @pl.when(jnp.logical_not(valid(k, 1)))
+            def _():
+                far_in[i * 9 + k] = jnp.zeros((SD, W), BF)
+
+        loop(far_take)
+        return dot_tn(kept[i], far_in[i * 9 : (i + 1) * 9].reshape(9 * SD, W))
+
+    part_other[...] = far_sum(1).astype(BF)
+    wait_part = to(part_other, part_in, 24, partner)
+    total = far_sum(0)
+    arrived([wait_part])
+    part_out[...] = (total + part_in[...].astype(F32)).astype(BF)
+    wait_far = to(part_out, far_back, 25, device(0, 0, far_same))
+
     acc_n[...] = jnp.zeros_like(acc_n)
 
     def back_take(k):
         @pl.when(valid(k, 1))
         def _():
-            await_bytes(rsem, 2, k, bd)
+            bd[k * 8 + far_same] = jnp.zeros((SD, W), BF)
+            bd[k * 8 + far_other] = jnp.zeros((SD, W), BF)
+            await_bytes(rsem, 2, k, bd, 6)
             rows = get_rows(bd, k, SD).astype(BF)
             acc_n[...] += dot(place(T_DEC_NODE, k, NODES, DROWS).astype(BF), rows)
 
     loop(back_take)
 
-    back_pre = acc_n[...].astype(BF)
+    arrived([wait_far])
+    back_pre = (acc_n[...] + far_back[...].astype(F32)).astype(BF)
     back_node = dot_nt(back_pre, w_msg[...])
     back_node_half = back_node.astype(BF)
     back_act = (dot_nt(back_node_half, w_down[...]) * slope(act[...])).astype(BF)
@@ -677,6 +726,13 @@
         v((2, NODES, W), BF),
         v((18, SD, W), BF),
         v((NODES, W), BF),
+        v((2, 9 * SD, NODES), BF),
+        v((18, SD, W), BF),
+        v((NODES, W), BF),
+        v((NODES, W), BF),
+        v((NODES, W), BF),
+        v((NODES, W), BF),
+        pltpu.SemaphoreType.DMA((2, 9)),
         v((72, SEP, W), BF),
         v((72, SEP, W), BF),
         v((72, SD, W), BF),

time: 132 us -> 139 us (1.053)
  Pallas kernels: 131 us -> 138 us
    pallas_call x1, Pallas kernels: 129 us -> 135 us  [on_device(): pl.pallas_call(kernel, out_shape=(jax.ShapeDtypeStruct((CELLS, W), BF),)...]
where the time goes in v4:
time: 139 us; the launch traced here: 138 us
  Pallas kernels  138 us (99%)
    pallas_call x1, Pallas kernels, on_device(): pl.pallas_call(kernel, out_shape=(jax.ShapeDtypeStruct((CELLS, W), BF),)...  135 us

profile of v4, /device:TPU:1, one launch (start us, length us, event | category | flops | bytes accessed | tf_op | source)
XLA Modules:
  0.0 138.4 jit_solution(6477844169791788111)
XLA Ops:
  0.6 135.3 %step.1 = (bf16[1024,512]{1,0:T(8,128)(2,1)}, f32[4,512]{1,0:T(4,128)}, f32[4,512]{1,0:T(4,128)}, f32[4,512]{1,0:T(4,128)}, f32[4,512]{1,0:T(4,128)}, /*index=5*/f32[4,512]{1,0:T(4,128)}, f32[4,84]{1,0:T(4,128)}) custom-call(s32[9,8,21]{2,1,0:T(8,128)} %bitcast.13, s32[9,8,21]{2,1,0:T(8,128)} %bitcast.14, s32[9,8,32]{2,1,0:T(8,128)} %bitcast.15, ...), custom_call_target="tpu_custom_call" | custom-call | tf_op jit(solution)/shard_map/step/pallas_call | solution.py:809
  135.9 2.5 %finish.1 = (f32[1024,512]{1,0:T(8,128)}, f32[4,512]{1,0:T(4,128)}, f32[4,512]{1,0:T(4,128)}, f32[4,512]{1,0:T(4,128)}, f32[4,512]{1,0:T(4,128)}, /*index=5*/f32[4,512]{1,0:T(4,128)}, f32[4,84]{1,0:T(4,128)}) custom-call(bf16[1024,512]{1,0:T(8,128)(2,1)} %get-tuple-element.14.refs_0_, f32[4,512]{1,0:T(4,128)} %get-tuple-element.15.refs_1_, ...), custom_call_target="tpu_custom_call" | custom-call | tf_op jit(solution)/shard_map/finish/pallas_call | solution.py:839

commit v5 on v3

--- a/solution.py
+++ b/solution.py
@@ -100,6 +100,8 @@
     cols,
     grid_grad,
     grid_half,
+    through,
+    base,
     os_,
     by_part,
     far_part,
@@ -379,9 +381,9 @@
     def enc_take(k):
         @pl.when(valid(k, -1))
         def _():
+            spread = place(T_ENC_NODE, k, NODES, EROWS).astype(BF)
             await_bytes(rsem, 0, k, ed)
-            rows = get_rows(ed, k, SEP).astype(BF)
-            acc_n[...] += dot(place(T_ENC_NODE, k, NODES, EROWS).astype(BF), rows)
+            acc_n[...] += dot(spread, get_rows(ed, k, SEP).astype(BF))
 
     loop(enc_take)
 
@@ -432,6 +434,9 @@
         loop(relay_send)
         dd[4 * 8 + source] = far_out[i * 9 + 4]
 
+    through[...] = dot_nt(wo[...], w_dec[...]).astype(BF)
+    base[...] = dot_nt(grid_latent[...], wo[...]) - target[...].T
+
     arrived(far_tables)
     arrived([far_block])
     far_block = to(far_rows.at[0], far_rows.at[1], 30, partner)
@@ -443,10 +448,11 @@
     def dec_take(k):
         @pl.when(valid(k, -1))
         def _():
+            spread = place(T_DEC_CELL, k, CELLS, DROWS).astype(BF)
+            weight = column(T_DEC_SCALE, k, DROWS)
             await_bytes(rsem, 1, k, dd)
             pre = get_rows(dd, k, SD)
-            rows = (column(T_DEC_SCALE, k, DROWS) * (pre * sigmoid(pre))).astype(BF)
-            acc_c[...] += dot(place(T_DEC_CELL, k, CELLS, DROWS).astype(BF), rows)
+            acc_c[...] += dot(spread, (weight * (pre * sigmoid(pre))).astype(BF))
 
     loop(dec_take)
 
@@ -454,17 +460,10 @@
         at = pl.ds(b * 256, 256)
         gathered = acc_c[at, :].astype(BF)
         gath[at, :] = gathered
-        blended = (grid_latent[at, :].astype(F32) + dot(gathered, w_dec[...])).astype(BF)
-        blend[at, :] = blended
-        output = dot_nt(blended, wo[...])
         weight = cols[0:256, T_AREA + b : T_AREA + b + 1]
-        residual = (weight * (output - target[:, at].T)).astype(BF)
+        residual = (weight * (base[at, :] + dot_nt(gathered, through[...]))).astype(BF)
         resid[at, :] = residual
-        back = dot(residual, wo[...])
-        grid_grad[at, :] = back
-        half = back.astype(BF)
-        bhalf[at, :] = half
-        bgath[at, :] = dot_nt(half, w_dec[...]).astype(BF)
+        bgath[at, :] = dot(residual, through[...]).astype(BF)
 
     def back_send(k):
         @pl.when(valid(k, -1))
@@ -476,6 +475,13 @@
             own(k, bs, bd)
 
     loop(back_send)
+
+    for b in range(4):
+        at = pl.ds(b * 256, 256)
+        blend[at, :] = (grid_latent[at, :].astype(F32) + dot(gath[at, :], w_dec[...])).astype(BF)
+        back = dot(resid[at, :], wo[...])
+        grid_grad[at, :] = back
+        bhalf[at, :] = back.astype(BF)
 
     def over_lat(src, dst, slot):
         return [
@@ -506,9 +512,9 @@
     def back_take(k):
         @pl.when(valid(k, 1))
         def _():
+            spread = place(T_DEC_NODE, k, NODES, DROWS).astype(BF)
             await_bytes(rsem, 2, k, bd)
-            rows = get_rows(bd, k, SD).astype(BF)
-            acc_n[...] += dot(place(T_DEC_NODE, k, NODES, DROWS).astype(BF), rows)
+            acc_n[...] += dot(spread, get_rows(bd, k, SD).astype(BF))
 
     loop(back_take)
 
@@ -588,11 +594,10 @@
     def enc_back_take(k):
         @pl.when(valid(k, 1))
         def _():
-            await_bytes(rsem, 3, k, fd)
-            rows = get_rows(fd, k, SEP).astype(BF)
             weight = table[pl.ds(T_ENC_SCALE + k, 1), :][:, 0:EROWS]
             spread = (place(T_ENC_CELL, k, CELLS, EROWS) * weight).astype(BF)
-            grid_grad[...] += dot(spread, rows)
+            await_bytes(rsem, 3, k, fd)
+            grid_grad[...] += dot(spread, get_rows(fd, k, SEP).astype(BF))
 
     loop(enc_back_take, 0, 8)
 
@@ -671,6 +676,8 @@
         v((256, 128), F32),
         v((CELLS, W), F32),
         v((CELLS, W), BF),
+        v((128, W), BF),
+        v((CELLS, 128), F32),
         pltpu.SemaphoreType.DMA((4,)),
         v((8, 16, 128), F32),
         v((2, 16, 128), F32),

time: 132 us -> 132 us (level)
  no operation moved by 1% of the time
where the time goes in v5:
time: 132 us; the launch traced here: 131 us
  Pallas kernels  131 us (99%)
    pallas_call x1, Pallas kernels, on_device(): pl.pallas_call(kernel, out_shape=(jax.ShapeDtypeStruct((CELLS, W), BF),)...  128 us

profile of v5, /device:TPU:1, one launch (start us, length us, event | category | flops | bytes accessed | tf_op | source)
XLA Modules:
  0.0 131.4 jit_solution(10401631653649231960)
XLA Ops:
  0.6 128.3 %step.1 = (bf16[1024,512]{1,0:T(8,128)(2,1)}, f32[4,512]{1,0:T(4,128)}, f32[4,512]{1,0:T(4,128)}, f32[4,512]{1,0:T(4,128)}, f32[4,512]{1,0:T(4,128)}, /*index=5*/f32[4,512]{1,0:T(4,128)}, f32[4,84]{1,0:T(4,128)}) custom-call(s32[9,8,21]{2,1,0:T(8,128)} %bitcast.13, s32[9,8,21]{2,1,0:T(8,128)} %bitcast.14, s32[9,8,32]{2,1,0:T(8,128)} %bitcast.15, ...), custom_call_target="tpu_custom_call" | custom-call | tf_op jit(solution)/shard_map/step/pallas_call | solution.py:760
  128.9 2.5 %finish.1 = (f32[1024,512]{1,0:T(8,128)}, f32[4,512]{1,0:T(4,128)}, f32[4,512]{1,0:T(4,128)}, f32[4,512]{1,0:T(4,128)}, f32[4,512]{1,0:T(4,128)}, /*index=5*/f32[4,512]{1,0:T(4,128)}, f32[4,84]{1,0:T(4,128)}) custom-call(bf16[1024,512]{1,0:T(8,128)(2,1)} %get-tuple-element.14.refs_0_, f32[4,512]{1,0:T(4,128)} %get-tuple-element.15.refs_1_, ...), custom_call_target="tpu_custom_call" | custom-call | tf_op jit(solution)/shard_map/finish/pallas_call | solution.py:790

commit v6 on v5

--- a/solution.py
+++ b/solution.py
@@ -448,11 +448,11 @@
     def dec_take(k):
         @pl.when(valid(k, -1))
         def _():
-            spread = place(T_DEC_CELL, k, CELLS, DROWS).astype(BF)
             weight = column(T_DEC_SCALE, k, DROWS)
             await_bytes(rsem, 1, k, dd)
             pre = get_rows(dd, k, SD)
-            acc_c[...] += dot(spread, (weight * (pre * sigmoid(pre))).astype(BF))
+            rows = (weight * (pre * sigmoid(pre))).astype(BF)
+            acc_c[...] += dot(place(T_DEC_CELL, k, CELLS, DROWS).astype(BF), rows)
 
     loop(dec_take)
 
@@ -594,10 +594,11 @@
     def enc_back_take(k):
         @pl.when(valid(k, 1))
         def _():
+            await_bytes(rsem, 3, k, fd)
+            rows = get_rows(fd, k, SEP).astype(BF)
             weight = table[pl.ds(T_ENC_SCALE + k, 1), :][:, 0:EROWS]
             spread = (place(T_ENC_CELL, k, CELLS, EROWS) * weight).astype(BF)
-            await_bytes(rsem, 3, k, fd)
-            grid_grad[...] += dot(spread, get_rows(fd, k, SEP).astype(BF))
+            grid_grad[...] += dot(spread, rows)
 
     loop(enc_back_take, 0, 8)
 

time: 132 us -> 130 us (0.985)
  no operation moved by 1% of the time
where the time goes in v6:
time: 130 us
  Pallas kernels  130 us (100%)
    pallas_call x1, Pallas kernels, on_device(): pl.pallas_call(kernel, out_shape=(jax.ShapeDtypeStruct((CELLS, W), BF),)...  127 us

profile of v6, /device:TPU:1, one launch (start us, length us, event | category | flops | bytes accessed | tf_op | source)
XLA Modules:
  0.0 130.3 jit_solution(7967278215273833325)
XLA Ops:
  0.6 127.1 %step.1 = (bf16[1024,512]{1,0:T(8,128)(2,1)}, f32[4,512]{1,0:T(4,128)}, f32[4,512]{1,0:T(4,128)}, f32[4,512]{1,0:T(4,128)}, f32[4,512]{1,0:T(4,128)}, /*index=5*/f32[4,512]{1,0:T(4,128)}, f32[4,84]{1,0:T(4,128)}) custom-call(s32[9,8,21]{2,1,0:T(8,128)} %bitcast.13, s32[9,8,21]{2,1,0:T(8,128)} %bitcast.14, s32[9,8,32]{2,1,0:T(8,128)} %bitcast.15, ...), custom_call_target="tpu_custom_call" | custom-call | tf_op jit(solution)/shard_map/step/pallas_call | solution.py:761
  127.8 2.5 %finish.1 = (f32[1024,512]{1,0:T(8,128)}, f32[4,512]{1,0:T(4,128)}, f32[4,512]{1,0:T(4,128)}, f32[4,512]{1,0:T(4,128)}, f32[4,512]{1,0:T(4,128)}, /*index=5*/f32[4,512]{1,0:T(4,128)}, f32[4,84]{1,0:T(4,128)}) custom-call(bf16[1024,512]{1,0:T(8,128)(2,1)} %get-tuple-element.14.refs_0_, f32[4,512]{1,0:T(4,128)} %get-tuple-element.15.refs_1_, ...), custom_call_target="tpu_custom_call" | custom-call | tf_op jit(solution)/shard_map/finish/pallas_call | solution.py:791
